TPU v7x, 32 devices: a whole 2x2x4 slice. The times are simulated.
32 devices in a mesh: gx: 2 (over core), gy: 4 (over y, x), gz: 4 (over z).
Axes of the slice: x: 2, y: 2, z: 4, core: 2. Of those that a mesh axis runs over, the one named last changes fastest.
Arguments:
- block_values: bfloat16 [4, 64, 4, 6, 128, 128], P('gy', 'gx', 'gz'), as said below
- block_cols: int32 [4, 64, 4, 6], P('gy', 'gx', 'gz'), may hold values from 0 to 63, as said below
Outputs:
- purified: float32 [256, 32768], P(('gx', 'gy'), 'gz')
Inputs may be any that keep to these rules, and one draw needn't show every extreme that they name: block_cols[a, s, b, :] holds 6 distinct tile columns of panel b at which tile row a * 64 + s of P is nonzero; every tile column of a panel is listed by exactly 6 tile rows of each slab; the pattern is symmetric: tile (i, j) is listed exactly when tile (j, i) is. `block_values`: P is symmetric: the tile listed at (i, j) is the transpose of the tile listed at (j, i), and diagonal tiles are symmetric.
All inputs are finite; a program needn't handle non-finite values.
Results may differ from a plain program's by a relative error of at most 0.0033.
Values may be sent and summed in bfloat16 or wider, within the bound.
No kernel may reach another device: no remote copies, remote signals or barrier semaphores. Data moves between devices by JAX's collectives and lax.ppermute only.
A program may use at most 128 MiB of HBM per device.

v0:
```python
import functools

import jax
import jax.numpy as jnp
from jax import lax
from jax.experimental import pallas as pl
from jax.experimental.pallas import tpu as pltpu
from jax.sharding import PartitionSpec as P

WIN = 1
UNROLL = 32
VMEM = pltpu.MemorySpace.VMEM
SMEM = pltpu.MemorySpace.SMEM


def limit(mib):
    return pltpu.CompilerParams(vmem_limit_bytes=mib << 20)


def assemble_kernel(parts, *refs):
    part_refs, out_ref, sems = refs[:parts], refs[parts], refs[parts + 1]
    here = part_refs[0].shape[0]
    copies = [
        pltpu.make_async_copy(part_refs[t], out_ref.at[pl.ds(t * here, here)], sems.at[t])
        for t in range(parts)
    ]
    for copy in copies:
        copy.start()
    for copy in copies:
        copy.wait()


def assemble(parts):
    here = parts[0].shape[0]
    shape = (here * len(parts),) + parts[0].shape[1:]
    return pl.pallas_call(
        functools.partial(assemble_kernel, len(parts)),
        out_shape=pltpu.VMEM(shape, jnp.bfloat16),
        in_specs=[pl.BlockSpec(memory_space=pltpu.HBM)] * len(parts),
        out_specs=pl.BlockSpec(memory_space=VMEM),
        scratch_shapes=[pltpu.SemaphoreType.DMA((len(parts),))],
        compiler_params=limit(46),
        cost_estimate=pl.CostEstimate(flops=4_000_000, bytes_accessed=25_000_000, transcendentals=0),
        name="assemble",
    )(*parts)


def pick_kernel(*refs):
    blocks = len(refs) // 2
    a, b = lax.axis_index("gy"), lax.axis_index("gz")
    for m in range(blocks):
        for k in range(blocks):

            @pl.when(a ^ b ^ k == m)
            def _(k=k, m=m):
                refs[blocks + k][...] = refs[m][...]


def pick(values):
    return pl.pallas_call(
        pick_kernel,
        out_shape=[jax.ShapeDtypeStruct(value.shape, value.dtype) for value in values],
        in_specs=[pl.BlockSpec(memory_space=VMEM)] * len(values),
        out_specs=[pl.BlockSpec(memory_space=VMEM)] * len(values),
        compiler_params=limit(8),
        cost_estimate=pl.CostEstimate(flops=1_000_000, bytes_accessed=2_000_000, transcendentals=0),
        name="pick",
    )(*values)


def swaps(size, step):
    return [(i, i ^ step) for i in range(size)]


def invert_kernel(cols_ref, inv_ref):
    rows, slots = cols_ref.shape
    count = rows * slots
    lane = lax.broadcasted_iota(jnp.int32, (rows, 128), 1)
    hits = jnp.concatenate(
        [(cols_ref[:, j : j + 1] == lane).astype(jnp.float32) for j in range(slots)], axis=0
    )
    above = lax.broadcasted_iota(jnp.int32, (count, count), 0) > lax.broadcasted_iota(
        jnp.int32, (count, count), 1
    )
    rank = jnp.dot(
        above.astype(jnp.bfloat16), hits.astype(jnp.bfloat16), preferred_element_type=jnp.float32
    )
    code = jnp.concatenate(
        [lax.broadcasted_iota(jnp.int32, (rows, 128), 0) * 8 + j for j in range(slots)], axis=0
    ).astype(jnp.float32)
    code = code * hits
    lines = [
        jnp.sum(jnp.where(rank == n, code, 0.0), axis=0, keepdims=True) for n in range(slots)
    ]
    lines += [jnp.zeros_like(lines[0])] * (8 - slots)
    inv_ref[...] = jnp.concatenate(lines, axis=0).astype(jnp.int32)


def invert(columns):
    return pl.pallas_call(
        invert_kernel,
        out_shape=jax.ShapeDtypeStruct((8, 128), jnp.int32),
        in_specs=[pl.BlockSpec(memory_space=VMEM)],
        out_specs=pl.BlockSpec(memory_space=VMEM),
        compiler_params=limit(4),
        cost_estimate=pl.CostEstimate(flops=4_000_000, bytes_accessed=4096, transcendentals=0),
        name="invert",
    )(columns)


def product_one_kernel(by_rows, lefts, parts, index_ref, *refs):
    left_refs, refs = refs[:lefts], refs[lefts:]
    part_refs, refs = refs[:parts], refs[parts:]
    blocks = len(refs) - 4
    send_refs, (left_ref, tile_ref, product_ref, sems) = refs[:blocks], refs[blocks:]
    g, a, b = lax.axis_index("gx"), lax.axis_index("gy"), lax.axis_index("gz")
    here, slots = part_refs[0].shape[:2]
    slab = here * parts
    rows = product_ref.shape[2]
    height = blocks * rows
    chosen = a ^ b if by_rows else a
    for k in range(lefts):

        @pl.when(chosen == k)
        def _(k=k):
            left_ref[...] = left_refs[k][...]

    tail = left_ref[pl.ds(slots * height, 16), :].astype(jnp.float32)
    columns = [jnp.max(tail[k : k + 1, :]).astype(jnp.int32) for k in range(slots)]
    targets = []
    for k in range(slots):
        if by_rows:
            p = lax.rem(columns[k] + slab - here * g, slab)
            targets.append([index_ref[p, j] for j in range(slots)])
            for t in range(parts):

                @pl.when(p // here == t)
                def _(k=k, t=t, p=p):
                    pltpu.make_async_copy(
                        part_refs[t].at[lax.rem(p, here)], tile_ref.at[k], sems.at[k, 0]
                    ).start()

        else:
            entries = [index_ref[n, columns[k]] for n in range(slots)]
            targets.append([entry >> 3 for entry in entries])
            for n in range(slots):
                p, j = entries[n] >> 3, entries[n] & 7
                for t in range(parts):

                    @pl.when(p // here == t)
                    def _(k=k, n=n, t=t, p=p, j=j):
                        pltpu.make_async_copy(
                            part_refs[t].at[lax.rem(p, here), j], tile_ref.at[k, n], sems.at[k, n]
                        ).start()

    lane = lax.broadcasted_iota(jnp.int32, (rows, left_ref.shape[1]), 1)
    places = jnp.zeros_like(lane)
    for k in range(slots):
        left = left_ref[pl.ds(k * height, height), :]
        if by_rows:
            pltpu.make_async_copy(part_refs[0].at[0], tile_ref.at[k], sems.at[k, 0]).wait()
        else:
            for n in range(slots):
                pltpu.make_async_copy(part_refs[0].at[0, 0], tile_ref.at[k, n], sems.at[k, n]).wait()
        for n in range(slots):
            product = lax.dot_general(
                left,
                tile_ref[k, n],
                (((1,), (0 if by_rows else 1,)), ((), ())),
                preferred_element_type=jnp.float32,
            ).astype(jnp.bfloat16)
            places = jnp.where(lane == k * slots + n, targets[k][n], places)
            for q in range(blocks):
                product_ref[q, k * slots + n] = product[q * rows : (q + 1) * rows]
    places = places.astype(jnp.float32).astype(jnp.bfloat16)
    me = a if by_rows else b
    for k in range(blocks):
        send_refs[k][pl.ds(0, slots * slots)] = product_ref[me ^ k]
        send_refs[k][slots * slots] = places


def product_one(by_rows, index, lefts, parts, blocks, height):
    slots, tile = parts[0].shape[1:3]
    rows = height // blocks
    message = jax.ShapeDtypeStruct((slots * slots + 1, rows, tile), jnp.bfloat16)
    return pl.pallas_call(
        functools.partial(product_one_kernel, by_rows, len(lefts), len(parts)),
        out_shape=[message] * blocks,
        in_specs=[pl.BlockSpec(memory_space=SMEM)]
        + [pl.BlockSpec(memory_space=VMEM)] * len(lefts)
        + [pl.BlockSpec(memory_space=pltpu.HBM)] * len(parts),
        out_specs=[pl.BlockSpec(memory_space=VMEM)] * blocks,
        scratch_shapes=[
            pltpu.VMEM(lefts[0].shape, jnp.bfloat16),
            pltpu.VMEM((slots, slots, tile, tile), jnp.bfloat16),
            pltpu.VMEM((blocks, slots * slots, rows, tile), jnp.bfloat16),
            pltpu.SemaphoreType.DMA((slots, slots)),
        ],
        compiler_params=limit(50),
        cost_estimate=pl.CostEstimate(flops=12_000_000, bytes_accessed=4_000_000, transcendentals=0),
        name="one_rows" if by_rows else "one_columns",
    )(index, *lefts, *parts)


def merge_kernel(*refs):
    sources = len(refs) - 5
    message_refs, (out_ref, acc_ref, vector_ref, place_ref, sem) = refs[:sources], refs[sources:]
    count = message_refs[0].shape[0] - 1
    lines = [ref[count].astype(jnp.float32)[0:1] for ref in message_refs]
    lines += [jnp.zeros_like(lines[0])] * (8 - sources)
    vector_ref[...] = jnp.concatenate(lines, axis=0).astype(jnp.int32)
    copy = pltpu.make_async_copy(vector_ref, place_ref, sem)
    copy.start()
    acc_ref[...] = jnp.zeros_like(acc_ref)
    copy.wait()
    for e in range(count):
        for s in range(sources):
            acc_ref[place_ref[s, e]] += message_refs[s][e].astype(jnp.float32)
    out_ref[...] = acc_ref[...].astype(jnp.bfloat16)


def merge(messages, slab):
    _, rows, tile = messages[0].shape
    return pl.pallas_call(
        merge_kernel,
        out_shape=jax.ShapeDtypeStruct((slab, rows, tile), jnp.bfloat16),
        in_specs=[pl.BlockSpec(memory_space=VMEM)] * len(messages),
        out_specs=pl.BlockSpec(memory_space=VMEM),
        scratch_shapes=[
            pltpu.VMEM((slab, rows, tile), jnp.float32),
            pltpu.VMEM((8, 128), jnp.int32),
            pltpu.SMEM((8, 128), jnp.int32),
            pltpu.SemaphoreType.DMA,
        ],
        compiler_params=limit(8),
        cost_estimate=pl.CostEstimate(flops=4_000_000, bytes_accessed=1_000_000, transcendentals=0),
        name="merge",
    )(*messages)


def product_two_kernel(by_rows, here, blocks, index_ref, slab_ref, *refs):
    round_refs, refs = refs[:blocks], refs[blocks:]
    send_refs, (left_ref,) = refs[:blocks], refs[blocks:]
    g, a, b = lax.axis_index("gx"), lax.axis_index("gy"), lax.axis_index("gz")
    slab, slots = slab_ref.shape[:2]
    rows = left_ref.shape[2]
    for k in range(blocks):
        left_ref[k if by_rows else a ^ b ^ k] = round_refs[k][...]
    extra = jnp.where(a == b, 3.0, 0.0).astype(jnp.float32)

    def left_of(p):
        return jnp.concatenate([left_ref[m, p] for m in range(blocks)], axis=0)

    def one(q, lefts, tiles, same):
        summed = None
        for n in range(0, slots, 2):
            left = jnp.concatenate([left_of(p) for p in lefts[n : n + 2]], axis=1)
            pair = jnp.concatenate(tiles[n : n + 2], axis=1 if by_rows else 0)
            if by_rows:
                first, second, contract = pair, left, 1
            else:
                first, second, contract = left, pair, 0
            product = lax.dot_general(
                first,
                second,
                (((1,), (contract,)), ((), ())),
                preferred_element_type=jnp.float32,
            )
            summed = product if summed is None else summed + product
        summed = summed.T if by_rows else summed
        for m in range(blocks):
            value = extra * left_ref[m, same].astype(jnp.float32) - 2.0 * summed[m * rows : (m + 1) * rows]
            send_refs[m][q] = value.astype(jnp.bfloat16)

    @pl.loop(0, slab, step=UNROLL)
    def _(first):
        for u in range(UNROLL):
            q = first + u
            entries = [index_ref[q, n] if by_rows else index_ref[n, q] for n in range(slots)]
            if by_rows:
                tiles = [slab_ref[q, j] for j in range(slots)]
                one(q, entries, tiles, lax.rem(q + here * g, slab))
            else:
                lefts = [entry >> 3 for entry in entries]
                tiles = [slab_ref[entry >> 3, entry & 7] for entry in entries]
                one(q, lefts, tiles, lax.rem(q + slab - here * g, slab))


def product_two(by_rows, index, rounded, tiles, here):
    slab, _, tile = tiles.shape[:3]
    blocks = len(rounded)
    rows = rounded[0].shape[1]
    message = jax.ShapeDtypeStruct((slab, rows, tile), jnp.bfloat16)
    return pl.pallas_call(
        functools.partial(product_two_kernel, by_rows, here, blocks),
        out_shape=[message] * blocks,
        in_specs=[pl.BlockSpec(memory_space=SMEM)]
        + [pl.BlockSpec(memory_space=VMEM)] * (1 + blocks),
        out_specs=[pl.BlockSpec(memory_space=VMEM)] * blocks,
        scratch_shapes=[pltpu.VMEM((blocks, slab, rows, tile), jnp.bfloat16)],
        compiler_params=limit(20),
        cost_estimate=pl.CostEstimate(flops=30_000_000, bytes_accessed=12_000_000, transcendentals=0),
        name="two_rows" if by_rows else "two_columns",
    )(index, tiles, *rounded)


def finish_kernel(here, *refs):
    half = len(refs) // 2
    first, second, out_ref = refs[:half], refs[half:-1], refs[-1]
    g = lax.axis_index("gx")
    slab, rows, tile = first[0].shape

    def add(refs_in, y):
        total = refs_in[0][y].astype(jnp.float32)
        for ref in refs_in[1:]:
            total = total + ref[y].astype(jnp.float32)
        return total

    @pl.loop(0, slab, unroll=8)
    def _(y):
        columns = pl.ds(pl.multiple_of(y * tile, tile), tile)
        out_ref[0:rows, columns] = add(first, y)
        out_ref[rows : 2 * rows, columns] = add(second, lax.rem(y + slab - here * g, slab))


def finish(first, second, here):
    slab, rows, tile = first[0].shape
    return pl.pallas_call(
        functools.partial(finish_kernel, here),
        out_shape=jax.ShapeDtypeStruct((2 * rows, slab * tile), jnp.float32),
        in_specs=[pl.BlockSpec(memory_space=VMEM)] * (len(first) + len(second)),
        out_specs=pl.BlockSpec(memory_space=VMEM),
        compiler_params=limit(8),
        name="finish",
    )(*first, *second)


def local(block_values, block_cols):
    tiles_here = block_values[0, :, 0]
    columns_here = block_cols[0, :, 0]
    here, slots, tile, _ = tiles_here.shape
    parts = lax.axis_size("gx")
    size = lax.axis_size("gy")
    blocks = WIN * tile // size
    rows = blocks // 2
    height = rows * size

    def payload(first):
        window = tiles_here[0].reshape(slots, size, blocks, tile)[:, :, first : first + rows]
        tail = jnp.broadcast_to(columns_here[0].astype(jnp.bfloat16)[:, None], (slots, tile))
        tail = jnp.pad(tail, ((0, 16 - slots), (0, 0)))
        return jnp.concatenate([window.reshape(slots * height, tile), tail], axis=0)

    pay_a, pay_b = payload(0), payload(rows)
    both = ("gy", "gz")
    shifts = [[((i + t) % parts, i) for i in range(parts)] for t in range(1, parts)]
    others = [lax.ppermute(columns_here, "gx", s) for s in shifts]
    moved = [lax.ppermute(tiles_here, "gx", s) for s in shifts]
    left_b = [
        lax.ppermute(pay_b, both, [(a, a * size + (a ^ k)) for a in range(size)]) for k in range(size)
    ]
    left_a = [pay_a] + [lax.ppermute(pay_a, "gy", [(0, k)]) for k in range(1, size)]
    columns = jnp.concatenate([columns_here] + others, axis=0)
    inverse = invert(columns)
    pieces = [tiles_here] + moved

    def scatter(sends, axis):
        return [sends[0]] + [lax.ppermute(sends[k], axis, swaps(size, k)) for k in range(1, size)]

    def spread(own, axis):
        return [own] + [lax.ppermute(own, axis, swaps(size, k)) for k in range(1, size)]

    sends_a = product_one(False, inverse, left_a, pieces, size, height)
    parts_a = scatter(sends_a, "gz")
    _, left_b = lax.optimization_barrier((sends_a[0], left_b))
    sends_b = product_one(True, columns, left_b, pieces, size, height)
    parts_b = scatter(sends_b, "gy")
    tiles = assemble(pieces)
    own_b = merge(parts_b, here * parts)
    own_a = merge(parts_a, here * parts)
    rounded_b = spread(own_b, "gy")
    rounded_a = spread(own_a, "gz")
    out_b = product_two(True, columns, rounded_b, tiles, here)
    crossed = scatter(out_b, "gy")
    picked = pick(crossed)
    got_b = scatter(picked, "gz")
    out_a = product_two(False, inverse, rounded_a, tiles, here)
    got_a = scatter(out_a, "gy")
    return finish(got_a, got_b, here)


def solution(mesh):
    in_specs = (P("gy", "gx", "gz", None, None, None), P("gy", "gx", "gz", None))
    out_specs = P(("gx", "gy"), "gz")
    return jax.shard_map(local, mesh=mesh, in_specs=in_specs, out_specs=out_specs, check_vma=False)
```

profile of v0, /device:TPU:0, one launch (start us, length us, event | category | flops | bytes accessed | tf_op | source)
XLA Modules:
  0.0 114.8 jit_solution(16249466908491910399)
XLA Ops:
  0.0 0.5 collective-permute-start.1
  0.5 0.9 slice.17
  1.4 0.8 fusion
  2.4 4.4 %collective-permute-start.2 = (bf16[400,128]{1,0:T(8,128)(2,1)S(1)}, bf16[400,128]{1,0:T(8,128)(2,1)S(1)}, u32[]{:S(2)}, u32[]{:S(2)}) collective-permute-start(bf16[400,128]{1,0:T(8,128)(2,1)S(1)} %get-tuple-element.56.refs_0_), channel_id=1, source_target_pairs={{0,4},{1,5},{2,6},{3,7},{16,20},{17,21},{18,22},{19,23}} | collective-permute-start | bytes 307208 | tf_op jit(solution)/shard_map/ppermute | solution.py:362
  6.8 1.3 %collective-permute-start.3 = (bf16[400,128]{1,0:T(8,128)(2,1)S(1)}, bf16[400,128]{1,0:T(8,128)(2,1)S(1)}, u32[]{:S(2)}, u32[]{:S(2)}) collective-permute-start(bf16[400,128]{1,0:T(8,128)(2,1)S(1)} %get-tuple-element.56.refs_0_), channel_id=1, source_target_pairs={{0,8},{1,9},{2,10},{3,11},{16,24},{17,25},{18,26},{19,27}} | collective-permute-start | bytes 307208 | tf_op jit(solution)/shard_map/ppermute | solution.py:362
  8.1 1.3 %collective-permute-start.4 = (bf16[400,128]{1,0:T(8,128)(2,1)S(1)}, bf16[400,128]{1,0:T(8,128)(2,1)S(1)}, u32[]{:S(2)}, u32[]{:S(2)}) collective-permute-start(bf16[400,128]{1,0:T(8,128)(2,1)S(1)} %get-tuple-element.56.refs_0_), channel_id=1, source_target_pairs={{0,12},{1,13},{2,14},{3,15},{16,28},{17,29},{18,30},{19,31}} | collective-permute-start | bytes 307208 | tf_op jit(solution)/shard_map/ppermute | solution.py:362
  9.4 0.7 copy.10
  10.1 0.2 collective-permute-start
  10.3 0.9 collective-permute-done
  11.3 0.7 collective-permute-start.14
  11.9 6.9 %collective-permute-start.15 = (bf16[400,128]{1,0:T(8,128)(2,1)S(1)}, bf16[400,128]{1,0:T(8,128)(2,1)S(1)}, u32[]{:S(2)}, u32[]{:S(2)}) collective-permute-start(bf16[400,128]{1,0:T(8,128)(2,1)S(1)} %get-tuple-element.55), channel_id=1, source_target_pairs={{0,1},{1,4},{2,11},{3,14},{16,17},{17,20},{18,27},{19,30}} | collective-permute-start | bytes 307208 | tf_op jit(solution)/shard_map/ppermute | solution.py:360
  18.9 2.7 %collective-permute-start.16 = (bf16[400,128]{1,0:T(8,128)(2,1)S(1)}, bf16[400,128]{1,0:T(8,128)(2,1)S(1)}, u32[]{:S(2)}, u32[]{:S(2)}) collective-permute-start(bf16[400,128]{1,0:T(8,128)(2,1)S(1)} %get-tuple-element.55), channel_id=1, source_target_pairs={{0,2},{1,7},{2,8},{3,13},{16,18},{17,23},{18,24},{19,29}} | collective-permute-start | bytes 307208 | tf_op jit(solution)/shard_map/ppermute | solution.py:360
  21.6 2.9 %collective-permute-start.17 = (bf16[400,128]{1,0:T(8,128)(2,1)S(1)}, bf16[400,128]{1,0:T(8,128)(2,1)S(1)}, u32[]{:S(2)}, u32[]{:S(2)}) collective-permute-start(bf16[400,128]{1,0:T(8,128)(2,1)S(1)} %get-tuple-element.55), channel_id=1, source_target_pairs={{0,3},{1,6},{2,9},{3,12},{16,19},{17,22},{18,25},{19,28}} | collective-permute-start | bytes 307208 | tf_op jit(solution)/shard_map/ppermute | solution.py:360
  24.7 0.4 invert.1.index_ref
  25.1 3.5 %one_columns.1 = (bf16[37,16,128]{2,1,0:T(8,128)(2,1)S(1)}, bf16[37,16,128]{2,1,0:T(8,128)(2,1)S(1)}, bf16[37,16,128]{2,1,0:T(8,128)(2,1)S(1)}, bf16[37,16,128]{2,1,0:T(8,128)(2,1)S(1)}) custom-call(s32[8,128]{1,0:T(8,128)S(1)} %invert.1.index_ref, bf16[400,128]{1,0:T(8,128)(2,1)S(1)} %get-tuple-element.56.refs_0_, ...), custom_call_target="tpu_custom_call" | custom-call | flops 12000000 | bytes 4000000 | tf_op jit(solution)/shard_map/one_columns/pallas_call | solution.py:186
  28.6 3.7 %one_rows.1 = (bf16[37,16,128]{2,1,0:T(8,128)(2,1)S(1)}, bf16[37,16,128]{2,1,0:T(8,128)(2,1)S(1)}, bf16[37,16,128]{2,1,0:T(8,128)(2,1)S(1)}, bf16[37,16,128]{2,1,0:T(8,128)(2,1)S(1)}) custom-call(s32[64,6]{1,0:T(8,128)S(1)} %copy.5.cols_ref.index_ref, bf16[400,128]{1,0:T(8,128)(2,1)S(1)} %collective-permute-done.14.refs_0_, ...), custom_call_target="tpu_custom_call" | custom-call | flops 12000000 | bytes 4000000 | tf_op jit(solution)/shard_map/one_rows/pallas_call | solution.py:186
  32.4 2.9 %collective-permute-start.19 = (bf16[37,16,128]{2,1,0:T(8,128)(2,1)S(1)}, bf16[37,16,128]{2,1,0:T(8,128)(2,1)S(1)}, u32[]{:S(2)}, u32[]{:S(2)}) collective-permute-start(bf16[37,16,128]{2,1,0:T(8,128)(2,1)S(1)} %get-tuple-element.43), channel_id=1, source_target_pairs={{0,8},{4,12},{8,0},{12,4},{1,9},{5,13},{9,1},{13,5},{2,10},{6,14},... | collective-permute-start | bytes 454664 | tf_op jit(solution)/shard_map/ppermute | solution.py:368
  35.3 1.1 collective-permute-start.20
  36.4 2.8 %collective-permute-done.18.refs_1_ = bf16[37,16,128]{2,1,0:T(8,128)(2,1)S(1)} collective-permute-done((bf16[37,16,128]{2,1,0:T(8,128)(2,1)S(1)}, bf16[37,16,128]{2,1,0:T(8,128)(2,1)S(1)}, u32[]{:S(2)}, u32[]{:S(2)}) %collective-permute-start.18) | collective-permute-done | bytes 151584 | tf_op jit(solution)/shard_map/ppermute | solution.py:368
  39.2 1.7 %collective-permute-done.19.refs_2_ = bf16[37,16,128]{2,1,0:T(8,128)(2,1)S(1)} collective-permute-done((bf16[37,16,128]{2,1,0:T(8,128)(2,1)S(1)}, bf16[37,16,128]{2,1,0:T(8,128)(2,1)S(1)}, u32[]{:S(2)}, u32[]{:S(2)}) %collective-permute-start.19) | collective-permute-done | bytes 151584 | tf_op jit(solution)/shard_map/ppermute | solution.py:368
  40.9 1.5 %collective-permute-done.20.refs_3_ = bf16[37,16,128]{2,1,0:T(8,128)(2,1)S(1)} collective-permute-done((bf16[37,16,128]{2,1,0:T(8,128)(2,1)S(1)}, bf16[37,16,128]{2,1,0:T(8,128)(2,1)S(1)}, u32[]{:S(2)}, u32[]{:S(2)}) %collective-permute-start.20) | collective-permute-done | bytes 151584 | tf_op jit(solution)/shard_map/ppermute | solution.py:368
  42.3 1.1 merge.3.refs_0_
  43.5 0.9 collective-permute-start.21
  44.4 2.1 %collective-permute-start.5 = (bf16[37,16,128]{2,1,0:T(8,128)(2,1)S(1)}, bf16[37,16,128]{2,1,0:T(8,128)(2,1)S(1)}, u32[]{:S(2)}, u32[]{:S(2)}) collective-permute-start(bf16[37,16,128]{2,1,0:T(8,128)(2,1)S(1)} %get-tuple-element.30), channel_id=1, source_target_pairs={{0,1},{1,0},{2,3},{3,2},{4,5},{5,4},{6,7},{7,6},{8,9},{9,8},{10,11... | collective-permute-start | bytes 454664 | tf_op jit(solution)/shard_map/ppermute | solution.py:368
  46.5 2.4 %collective-permute-start.7 = (bf16[37,16,128]{2,1,0:T(8,128)(2,1)S(1)}, bf16[37,16,128]{2,1,0:T(8,128)(2,1)S(1)}, u32[]{:S(2)}, u32[]{:S(2)}) collective-permute-start(bf16[37,16,128]{2,1,0:T(8,128)(2,1)S(1)} %get-tuple-element.32), channel_id=1, source_target_pairs={{0,3},{1,2},{2,1},{3,0},{4,7},{5,6},{6,5},{7,4},{8,11},{9,10},{10,... | collective-permute-start | bytes 454664 | tf_op jit(solution)/shard_map/ppermute | solution.py:368
  48.8 1.7 %collective-permute-start.22 = (bf16[64,16,128]{2,1,0:T(8,128)(2,1)S(1)}, bf16[64,16,128]{2,1,0:T(8,128)(2,1)S(1)}, u32[]{:S(2)}, u32[]{:S(2)}) collective-permute-start(bf16[64,16,128]{2,1,0:T(8,128)(2,1)S(1)} %merge.3.refs_0_), channel_id=1, source_target_pairs={{0,8},{4,12},{8,0},{12,4},{1,9},{5,13},{9,1},{13,5},{2,10},{6,14},... | collective-permute-start | bytes 786440 | tf_op jit(solution)/shard_map/ppermute | solution.py:371
  50.5 0.4 collective-permute-done.5.refs_1_
  51.0 1.3 %collective-permute-start.23 = (bf16[64,16,128]{2,1,0:T(8,128)(2,1)S(1)}, bf16[64,16,128]{2,1,0:T(8,128)(2,1)S(1)}, u32[]{:S(2)}, u32[]{:S(2)}) collective-permute-start(bf16[64,16,128]{2,1,0:T(8,128)(2,1)S(1)} %merge.3.refs_0_), channel_id=1, source_target_pairs={{0,12},{4,8},{8,4},{12,0},{1,13},{5,9},{9,5},{13,1},{2,14},{6,10},... | collective-permute-start | bytes 786440 | tf_op jit(solution)/shard_map/ppermute | solution.py:371
  52.3 6.8 %collective-permute-done.6.refs_2_ = bf16[37,16,128]{2,1,0:T(8,128)(2,1)S(1)} collective-permute-done((bf16[37,16,128]{2,1,0:T(8,128)(2,1)S(1)}, bf16[37,16,128]{2,1,0:T(8,128)(2,1)S(1)}, u32[]{:S(2)}, u32[]{:S(2)}) %collective-permute-start.6) | collective-permute-done | bytes 151584 | tf_op jit(solution)/shard_map/ppermute | solution.py:368
  59.1 1.1 merge.2.refs_0_
  60.2 1.4 %collective-permute-start.10 = (bf16[64,16,128]{2,1,0:T(8,128)(2,1)S(1)}, bf16[64,16,128]{2,1,0:T(8,128)(2,1)S(1)}, u32[]{:S(2)}, u32[]{:S(2)}) collective-permute-start(bf16[64,16,128]{2,1,0:T(8,128)(2,1)S(1)} %merge.2.refs_0_), channel_id=1, source_target_pairs={{0,3},{1,2},{2,1},{3,0},{4,7},{5,6},{6,5},{7,4},{8,11},{9,10},{10,... | collective-permute-start | bytes 786440 | tf_op jit(solution)/shard_map/ppermute | solution.py:371
  61.6 4.7 %collective-permute-start.8 = (bf16[64,16,128]{2,1,0:T(8,128)(2,1)S(1)}, bf16[64,16,128]{2,1,0:T(8,128)(2,1)S(1)}, u32[]{:S(2)}, u32[]{:S(2)}) collective-permute-start(bf16[64,16,128]{2,1,0:T(8,128)(2,1)S(1)} %merge.2.refs_0_), channel_id=1, source_target_pairs={{0,1},{1,0},{2,3},{3,2},{4,5},{5,4},{6,7},{7,6},{8,9},{9,8},{10,11... | collective-permute-start | bytes 786440 | tf_op jit(solution)/shard_map/ppermute | solution.py:371
  66.3 0.5 collective-permute-start.9
  66.8 4.6 %assemble.1.slab_ref = bf16[64,6,128,128]{3,2,1,0:T(8,128)(2,1)S(1)} custom-call(bf16[32,6,128,128]{3,2,1,0:T(8,128)(2,1)} %bitcast.10, bf16[32,6,128,128]{3,2,1,0:T(8,128)(2,1)} %collective-permute-done.1.refs_1_.refs_5_), custom_call_target="tpu_custom_call" | custom-call | flops 4000000 | bytes 25000000 | tf_op jit(solution)/shard_map/assemble/pallas_call | solution.py:36
  71.4 4.9 %two_rows.1 = (bf16[64,16,128]{2,1,0:T(8,128)(2,1)S(1)}, bf16[64,16,128]{2,1,0:T(8,128)(2,1)S(1)}, bf16[64,16,128]{2,1,0:T(8,128)(2,1)S(1)}, bf16[64,16,128]{2,1,0:T(8,128)(2,1)S(1)}) custom-call(s32[64,6]{1,0:T(8,128)S(1)} %copy.5.cols_ref.index_ref, bf16[64,6,128,128]{3,2,1,0:T(8,128)(2,1)S(1)} %assemble.1.slab_ref, ...), custom_call_target="tpu_custom_call" | custom-call | flops 30000000 | bytes 12000000 | tf_op jit(solution)/shard_map/two_rows/pallas_call | solution.py:294
  76.5 3.4 %collective-permute-start.26 = (bf16[64,16,128]{2,1,0:T(8,128)(2,1)S(1)}, bf16[64,16,128]{2,1,0:T(8,128)(2,1)S(1)}, u32[]{:S(2)}, u32[]{:S(2)}) collective-permute-start(bf16[64,16,128]{2,1,0:T(8,128)(2,1)S(1)} %get-tuple-element.48), channel_id=1, source_target_pairs={{0,12},{4,8},{8,4},{12,0},{1,13},{5,9},{9,5},{13,1},{2,14},{6,10},... | collective-permute-start | bytes 786440 | tf_op jit(solution)/shard_map/ppermute | solution.py:368
  79.9 5.5 %collective-permute-done.9.refs_2_ = bf16[64,16,128]{2,1,0:T(8,128)(2,1)S(1)} collective-permute-done((bf16[64,16,128]{2,1,0:T(8,128)(2,1)S(1)}, bf16[64,16,128]{2,1,0:T(8,128)(2,1)S(1)}, u32[]{:S(2)}, u32[]{:S(2)}) %collective-permute-start.9) | collective-permute-done | bytes 262176 | tf_op jit(solution)/shard_map/ppermute | solution.py:371
  85.3 2.9 %two_columns.1 = (bf16[64,16,128]{2,1,0:T(8,128)(2,1)S(1)}, bf16[64,16,128]{2,1,0:T(8,128)(2,1)S(1)}, bf16[64,16,128]{2,1,0:T(8,128)(2,1)S(1)}, bf16[64,16,128]{2,1,0:T(8,128)(2,1)S(1)}) custom-call(s32[8,128]{1,0:T(8,128)S(1)} %invert.1.index_ref, bf16[64,6,128,128]{3,2,1,0:T(8,128)(2,1)S(1)} %assemble.1.slab_ref, bf16[64,16,128]{2,1,0:T(8,128)(2,1)S(1)} %merge.2.refs_0_, ...), custom_call_target="tpu_custom_call" | custom-call | flops 30000000 | bytes 12000000 | tf_op jit(solution)/shard_map/two_columns/pallas_call | solution.py:294
  88.3 2.0 %collective-permute-start.12 = (bf16[64,16,128]{2,1,0:T(8,128)(2,1)S(1)}, bf16[64,16,128]{2,1,0:T(8,128)(2,1)S(1)}, u32[]{:S(2)}, u32[]{:S(2)}) collective-permute-start(bf16[64,16,128]{2,1,0:T(8,128)(2,1)S(1)} %get-tuple-element.35), channel_id=1, source_target_pairs={{0,8},{4,12},{8,0},{12,4},{1,9},{5,13},{9,1},{13,5},{2,10},{6,14},... | collective-permute-start | bytes 786440 | tf_op jit(solution)/shard_map/ppermute | solution.py:368
  90.3 1.5 %collective-permute-start.13 = (bf16[64,16,128]{2,1,0:T(8,128)(2,1)S(1)}, bf16[64,16,128]{2,1,0:T(8,128)(2,1)S(1)}, u32[]{:S(2)}, u32[]{:S(2)}) collective-permute-start(bf16[64,16,128]{2,1,0:T(8,128)(2,1)S(1)} %get-tuple-element.36), channel_id=1, source_target_pairs={{0,12},{4,8},{8,4},{12,0},{1,13},{5,9},{9,5},{13,1},{2,14},{6,10},... | collective-permute-start | bytes 786440 | tf_op jit(solution)/shard_map/ppermute | solution.py:368
  92.0 1.9 %collective-permute-start.28 = (bf16[64,16,128]{2,1,0:T(8,128)(2,1)S(1)}, bf16[64,16,128]{2,1,0:T(8,128)(2,1)S(1)}, u32[]{:S(2)}, u32[]{:S(2)}) collective-permute-start(bf16[64,16,128]{2,1,0:T(8,128)(2,1)S(1)} %get-tuple-element.51), channel_id=1, source_target_pairs={{0,2},{1,3},{2,0},{3,1},{4,6},{5,7},{6,4},{7,5},{8,10},{9,11},{10,... | collective-permute-start | bytes 786440 | tf_op jit(solution)/shard_map/ppermute | solution.py:368
  93.9 3.6 %collective-permute-done.11.refs_1_ = bf16[64,16,128]{2,1,0:T(8,128)(2,1)S(1)} collective-permute-done((bf16[64,16,128]{2,1,0:T(8,128)(2,1)S(1)}, bf16[64,16,128]{2,1,0:T(8,128)(2,1)S(1)}, u32[]{:S(2)}, u32[]{:S(2)}) %collective-permute-start.11) | collective-permute-done | bytes 262176 | tf_op jit(solution)/shard_map/ppermute | solution.py:368
  97.5 1.3 %collective-permute-start.29 = (bf16[64,16,128]{2,1,0:T(8,128)(2,1)S(1)}, bf16[64,16,128]{2,1,0:T(8,128)(2,1)S(1)}, u32[]{:S(2)}, u32[]{:S(2)}) collective-permute-start(bf16[64,16,128]{2,1,0:T(8,128)(2,1)S(1)} %get-tuple-element.52), channel_id=1, source_target_pairs={{0,3},{1,2},{2,1},{3,0},{4,7},{5,6},{6,5},{7,4},{8,11},{9,10},{10,... | collective-permute-start | bytes 786440 | tf_op jit(solution)/shard_map/ppermute | solution.py:368
  98.8 2.5 %collective-permute-done.12.refs_2_ = bf16[64,16,128]{2,1,0:T(8,128)(2,1)S(1)} collective-permute-done((bf16[64,16,128]{2,1,0:T(8,128)(2,1)S(1)}, bf16[64,16,128]{2,1,0:T(8,128)(2,1)S(1)}, u32[]{:S(2)}, u32[]{:S(2)}) %collective-permute-start.12) | collective-permute-done | bytes 262176 | tf_op jit(solution)/shard_map/ppermute | solution.py:368
  101.3 1.4 %collective-permute-done.13.refs_3_ = bf16[64,16,128]{2,1,0:T(8,128)(2,1)S(1)} collective-permute-done((bf16[64,16,128]{2,1,0:T(8,128)(2,1)S(1)}, bf16[64,16,128]{2,1,0:T(8,128)(2,1)S(1)}, u32[]{:S(2)}, u32[]{:S(2)}) %collective-permute-start.13) | collective-permute-done | bytes 262176 | tf_op jit(solution)/shard_map/ppermute | solution.py:368
  102.7 0.2 collective-permute-done.27.refs_5_
  102.9 10.4 %collective-permute-done.28.refs_6_ = bf16[64,16,128]{2,1,0:T(8,128)(2,1)S(1)} collective-permute-done((bf16[64,16,128]{2,1,0:T(8,128)(2,1)S(1)}, bf16[64,16,128]{2,1,0:T(8,128)(2,1)S(1)}, u32[]{:S(2)}, u32[]{:S(2)}) %collective-permute-start.28) | collective-permute-done | bytes 262176 | tf_op jit(solution)/shard_map/ppermute | solution.py:368
  113.4 1.4 %finish.1 = f32[32,8192]{1,0:T(8,128)} custom-call(bf16[64,16,128]{2,1,0:T(8,128)(2,1)S(1)} %get-tuple-element.33.refs_0_, bf16[64,16,128]{2,1,0:T(8,128)(2,1)S(1)} %collective-permute-done.11.refs_1_, bf16[64,16,128]{2,1,0:T(8,128)(2,1)S(1)} %collective-permute-done.12.refs_2_, bf16[64,16,128]{2,1,0:T(8,128)(2,1)S(1)} %collective-permute-done.13.refs_3_, ...), custom_call_target="tpu_custom_call" | custom-call | tf_op jit(solution)/shard_map/finish/pallas_call | solution.py:328
  (30 shorter events, 0.9 us)
Async XLA Ops:
  0.0 25.1 %collective-permute-start.1 = (bf16[32,6,128,128]{3,2,1,0:T(8,128)(2,1)}, bf16[32,6,128,128]{3,2,1,0:T(8,128)(2,1)}, u32[]{:S(2)}, u32[]{:S(2)}) collective-permute-start(bf16[32,6,128,128]{3,2,1,0:T(8,128)(2,1)} %bitcast.7), channel_id=1, source_target_pairs={{16,0},{0,16},{17,1},{1,17},{18,2},{2,18},{19,3},{3,19},{20,4},{4,... | collective-permute-start | bytes 18874376 | tf_op jit(solution)/shard_map/ppermute | solution.py:358
  2.4 9.5 %collective-permute-start.2 = (bf16[400,128]{1,0:T(8,128)(2,1)S(1)}, bf16[400,128]{1,0:T(8,128)(2,1)S(1)}, u32[]{:S(2)}, u32[]{:S(2)}) collective-permute-start(bf16[400,128]{1,0:T(8,128)(2,1)S(1)} %get-tuple-element.56.refs_0_), channel_id=1, source_target_pairs={{0,4},{1,5},{2,6},{3,7},{16,20},{17,21},{18,22},{19,23}} | collective-permute-start | bytes 307208 | tf_op jit(solution)/shard_map/ppermute | solution.py:362
  6.8 12.1 %collective-permute-start.3 = (bf16[400,128]{1,0:T(8,128)(2,1)S(1)}, bf16[400,128]{1,0:T(8,128)(2,1)S(1)}, u32[]{:S(2)}, u32[]{:S(2)}) collective-permute-start(bf16[400,128]{1,0:T(8,128)(2,1)S(1)} %get-tuple-element.56.refs_0_), channel_id=1, source_target_pairs={{0,8},{1,9},{2,10},{3,11},{16,24},{17,25},{18,26},{19,27}} | collective-permute-start | bytes 307208 | tf_op jit(solution)/shard_map/ppermute | solution.py:362
  8.1 13.5 %collective-permute-start.4 = (bf16[400,128]{1,0:T(8,128)(2,1)S(1)}, bf16[400,128]{1,0:T(8,128)(2,1)S(1)}, u32[]{:S(2)}, u32[]{:S(2)}) collective-permute-start(bf16[400,128]{1,0:T(8,128)(2,1)S(1)} %get-tuple-element.56.refs_0_), channel_id=1, source_target_pairs={{0,12},{1,13},{2,14},{3,15},{16,28},{17,29},{18,30},{19,31}} | collective-permute-start | bytes 307208 | tf_op jit(solution)/shard_map/ppermute | solution.py:362
  10.1 1.2 %collective-permute-start = (s32[32,6]{0,1:T(8,128)S(1)}, s32[32,6]{0,1:T(8,128)S(1)}, u32[]{:S(2)}, u32[]{:S(2)}) collective-permute-start(s32[32,6]{0,1:T(8,128)S(1)} %bitcast.14), channel_id=1, source_target_pairs={{16,0},{0,16},{17,1},{1,17},{18,2},{2,18},{19,3},{3,19},{20,4},{4,... | collective-permute-start | bytes 2312 | tf_op jit(solution)/shard_map/ppermute | solution.py:357
  11.3 17.3 %collective-permute-start.14 = (bf16[400,128]{1,0:T(8,128)(2,1)S(1)}, bf16[400,128]{1,0:T(8,128)(2,1)S(1)}, u32[]{:S(2)}, u32[]{:S(2)}) collective-permute-start(bf16[400,128]{1,0:T(8,128)(2,1)S(1)} %get-tuple-element.55), channel_id=1, source_target_pairs={{0,0},{1,5},{2,10},{3,15},{16,16},{17,21},{18,26},{19,31}} | collective-permute-start | bytes 307208 | tf_op jit(solution)/shard_map/ppermute | solution.py:360
  11.9 16.6 %collective-permute-start.15 = (bf16[400,128]{1,0:T(8,128)(2,1)S(1)}, bf16[400,128]{1,0:T(8,128)(2,1)S(1)}, u32[]{:S(2)}, u32[]{:S(2)}) collective-permute-start(bf16[400,128]{1,0:T(8,128)(2,1)S(1)} %get-tuple-element.55), channel_id=1, source_target_pairs={{0,1},{1,4},{2,11},{3,14},{16,17},{17,20},{18,27},{19,30}} | collective-permute-start | bytes 307208 | tf_op jit(solution)/shard_map/ppermute | solution.py:360
  18.9 9.7 %collective-permute-start.16 = (bf16[400,128]{1,0:T(8,128)(2,1)S(1)}, bf16[400,128]{1,0:T(8,128)(2,1)S(1)}, u32[]{:S(2)}, u32[]{:S(2)}) collective-permute-start(bf16[400,128]{1,0:T(8,128)(2,1)S(1)} %get-tuple-element.55), channel_id=1, source_target_pairs={{0,2},{1,7},{2,8},{3,13},{16,18},{17,23},{18,24},{19,29}} | collective-permute-start | bytes 307208 | tf_op jit(solution)/shard_map/ppermute | solution.py:360
  21.6 7.0 %collective-permute-start.17 = (bf16[400,128]{1,0:T(8,128)(2,1)S(1)}, bf16[400,128]{1,0:T(8,128)(2,1)S(1)}, u32[]{:S(2)}, u32[]{:S(2)}) collective-permute-start(bf16[400,128]{1,0:T(8,128)(2,1)S(1)} %get-tuple-element.55), channel_id=1, source_target_pairs={{0,3},{1,6},{2,9},{3,12},{16,19},{17,22},{18,25},{19,28}} | collective-permute-start | bytes 307208 | tf_op jit(solution)/shard_map/ppermute | solution.py:360
  32.3 6.9 %collective-permute-start.18 = (bf16[37,16,128]{2,1,0:T(8,128)(2,1)S(1)}, bf16[37,16,128]{2,1,0:T(8,128)(2,1)S(1)}, u32[]{:S(2)}, u32[]{:S(2)}) collective-permute-start(bf16[37,16,128]{2,1,0:T(8,128)(2,1)S(1)} %get-tuple-element.42), channel_id=1, source_target_pairs={{0,4},{4,0},{8,12},{12,8},{1,5},{5,1},{9,13},{13,9},{2,6},{6,2},{1... | collective-permute-start | bytes 454664 | tf_op jit(solution)/shard_map/ppermute | solution.py:368
  32.4 8.5 %collective-permute-start.19 = (bf16[37,16,128]{2,1,0:T(8,128)(2,1)S(1)}, bf16[37,16,128]{2,1,0:T(8,128)(2,1)S(1)}, u32[]{:S(2)}, u32[]{:S(2)}) collective-permute-start(bf16[37,16,128]{2,1,0:T(8,128)(2,1)S(1)} %get-tuple-element.43), channel_id=1, source_target_pairs={{0,8},{4,12},{8,0},{12,4},{1,9},{5,13},{9,1},{13,5},{2,10},{6,14},... | collective-permute-start | bytes 454664 | tf_op jit(solution)/shard_map/ppermute | solution.py:368
  35.3 7.0 %collective-permute-start.20 = (bf16[37,16,128]{2,1,0:T(8,128)(2,1)S(1)}, bf16[37,16,128]{2,1,0:T(8,128)(2,1)S(1)}, u32[]{:S(2)}, u32[]{:S(2)}) collective-permute-start(bf16[37,16,128]{2,1,0:T(8,128)(2,1)S(1)} %get-tuple-element.44), channel_id=1, source_target_pairs={{0,12},{4,8},{8,4},{12,0},{1,13},{5,9},{9,5},{13,1},{2,14},{6,10},... | collective-permute-start | bytes 454664 | tf_op jit(solution)/shard_map/ppermute | solution.py:368
  43.5 22.8 %collective-permute-start.21 = (bf16[64,16,128]{2,1,0:T(8,128)(2,1)S(1)}, bf16[64,16,128]{2,1,0:T(8,128)(2,1)S(1)}, u32[]{:S(2)}, u32[]{:S(2)}) collective-permute-start(bf16[64,16,128]{2,1,0:T(8,128)(2,1)S(1)} %merge.3.refs_0_), channel_id=1, source_target_pairs={{0,4},{4,0},{8,12},{12,8},{1,5},{5,1},{9,13},{13,9},{2,6},{6,2},{1... | collective-permute-start | bytes 786440 | tf_op jit(solution)/shard_map/ppermute | solution.py:371
  44.4 6.6 %collective-permute-start.5 = (bf16[37,16,128]{2,1,0:T(8,128)(2,1)S(1)}, bf16[37,16,128]{2,1,0:T(8,128)(2,1)S(1)}, u32[]{:S(2)}, u32[]{:S(2)}) collective-permute-start(bf16[37,16,128]{2,1,0:T(8,128)(2,1)S(1)} %get-tuple-element.30), channel_id=1, source_target_pairs={{0,1},{1,0},{2,3},{3,2},{4,5},{5,4},{6,7},{7,6},{8,9},{9,8},{10,11... | collective-permute-start | bytes 454664 | tf_op jit(solution)/shard_map/ppermute | solution.py:368
  46.5 12.6 %collective-permute-start.6 = (bf16[37,16,128]{2,1,0:T(8,128)(2,1)S(1)}, bf16[37,16,128]{2,1,0:T(8,128)(2,1)S(1)}, u32[]{:S(2)}, u32[]{:S(2)}) collective-permute-start(bf16[37,16,128]{2,1,0:T(8,128)(2,1)S(1)} %get-tuple-element.31), channel_id=1, source_target_pairs={{0,2},{1,3},{2,0},{3,1},{4,6},{5,7},{6,4},{7,5},{8,10},{9,11},{10,... | collective-permute-start | bytes 454664 | tf_op jit(solution)/shard_map/ppermute | solution.py:368
  46.5 12.6 %collective-permute-start.7 = (bf16[37,16,128]{2,1,0:T(8,128)(2,1)S(1)}, bf16[37,16,128]{2,1,0:T(8,128)(2,1)S(1)}, u32[]{:S(2)}, u32[]{:S(2)}) collective-permute-start(bf16[37,16,128]{2,1,0:T(8,128)(2,1)S(1)} %get-tuple-element.32), channel_id=1, source_target_pairs={{0,3},{1,2},{2,1},{3,0},{4,7},{5,6},{6,5},{7,4},{8,11},{9,10},{10,... | collective-permute-start | bytes 454664 | tf_op jit(solution)/shard_map/ppermute | solution.py:368
  48.8 22.6 %collective-permute-start.22 = (bf16[64,16,128]{2,1,0:T(8,128)(2,1)S(1)}, bf16[64,16,128]{2,1,0:T(8,128)(2,1)S(1)}, u32[]{:S(2)}, u32[]{:S(2)}) collective-permute-start(bf16[64,16,128]{2,1,0:T(8,128)(2,1)S(1)} %merge.3.refs_0_), channel_id=1, source_target_pairs={{0,8},{4,12},{8,0},{12,4},{1,9},{5,13},{9,1},{13,5},{2,10},{6,14},... | collective-permute-start | bytes 786440 | tf_op jit(solution)/shard_map/ppermute | solution.py:371
  51.0 20.4 %collective-permute-start.23 = (bf16[64,16,128]{2,1,0:T(8,128)(2,1)S(1)}, bf16[64,16,128]{2,1,0:T(8,128)(2,1)S(1)}, u32[]{:S(2)}, u32[]{:S(2)}) collective-permute-start(bf16[64,16,128]{2,1,0:T(8,128)(2,1)S(1)} %merge.3.refs_0_), channel_id=1, source_target_pairs={{0,12},{4,8},{8,4},{12,0},{1,13},{5,9},{9,5},{13,1},{2,14},{6,10},... | collective-permute-start | bytes 786440 | tf_op jit(solution)/shard_map/ppermute | solution.py:371
  60.2 16.2 %collective-permute-start.10 = (bf16[64,16,128]{2,1,0:T(8,128)(2,1)S(1)}, bf16[64,16,128]{2,1,0:T(8,128)(2,1)S(1)}, u32[]{:S(2)}, u32[]{:S(2)}) collective-permute-start(bf16[64,16,128]{2,1,0:T(8,128)(2,1)S(1)} %merge.2.refs_0_), channel_id=1, source_target_pairs={{0,3},{1,2},{2,1},{3,0},{4,7},{5,6},{6,5},{7,4},{8,11},{9,10},{10,... | collective-permute-start | bytes 786440 | tf_op jit(solution)/shard_map/ppermute | solution.py:371
  61.6 18.2 %collective-permute-start.8 = (bf16[64,16,128]{2,1,0:T(8,128)(2,1)S(1)}, bf16[64,16,128]{2,1,0:T(8,128)(2,1)S(1)}, u32[]{:S(2)}, u32[]{:S(2)}) collective-permute-start(bf16[64,16,128]{2,1,0:T(8,128)(2,1)S(1)} %merge.2.refs_0_), channel_id=1, source_target_pairs={{0,1},{1,0},{2,3},{3,2},{4,5},{5,4},{6,7},{7,6},{8,9},{9,8},{10,11... | collective-permute-start | bytes 786440 | tf_op jit(solution)/shard_map/ppermute | solution.py:371
  66.3 19.0 %collective-permute-start.9 = (bf16[64,16,128]{2,1,0:T(8,128)(2,1)S(1)}, bf16[64,16,128]{2,1,0:T(8,128)(2,1)S(1)}, u32[]{:S(2)}, u32[]{:S(2)}) collective-permute-start(bf16[64,16,128]{2,1,0:T(8,128)(2,1)S(1)} %merge.2.refs_0_), channel_id=1, source_target_pairs={{0,2},{1,3},{2,0},{3,1},{4,6},{5,7},{6,4},{7,5},{8,10},{9,11},{10,... | collective-permute-start | bytes 786440 | tf_op jit(solution)/shard_map/ppermute | solution.py:371
  76.3 13.9 %collective-permute-start.24 = (bf16[64,16,128]{2,1,0:T(8,128)(2,1)S(1)}, bf16[64,16,128]{2,1,0:T(8,128)(2,1)S(1)}, u32[]{:S(2)}, u32[]{:S(2)}) collective-permute-start(bf16[64,16,128]{2,1,0:T(8,128)(2,1)S(1)} %get-tuple-element.46), channel_id=1, source_target_pairs={{0,4},{4,0},{8,12},{12,8},{1,5},{5,1},{9,13},{13,9},{2,6},{6,2},{1... | collective-permute-start | bytes 786440 | tf_op jit(solution)/shard_map/ppermute | solution.py:368
  76.4 15.4 %collective-permute-start.25 = (bf16[64,16,128]{2,1,0:T(8,128)(2,1)S(1)}, bf16[64,16,128]{2,1,0:T(8,128)(2,1)S(1)}, u32[]{:S(2)}, u32[]{:S(2)}) collective-permute-start(bf16[64,16,128]{2,1,0:T(8,128)(2,1)S(1)} %get-tuple-element.47), channel_id=1, source_target_pairs={{0,8},{4,12},{8,0},{12,4},{1,9},{5,13},{9,1},{13,5},{2,10},{6,14},... | collective-permute-start | bytes 786440 | tf_op jit(solution)/shard_map/ppermute | solution.py:368
  76.5 15.3 %collective-permute-start.26 = (bf16[64,16,128]{2,1,0:T(8,128)(2,1)S(1)}, bf16[64,16,128]{2,1,0:T(8,128)(2,1)S(1)}, u32[]{:S(2)}, u32[]{:S(2)}) collective-permute-start(bf16[64,16,128]{2,1,0:T(8,128)(2,1)S(1)} %get-tuple-element.48), channel_id=1, source_target_pairs={{0,12},{4,8},{8,4},{12,0},{1,13},{5,9},{9,5},{13,1},{2,14},{6,10},... | collective-permute-start | bytes 786440 | tf_op jit(solution)/shard_map/ppermute | solution.py:368
  88.2 9.2 %collective-permute-start.11 = (bf16[64,16,128]{2,1,0:T(8,128)(2,1)S(1)}, bf16[64,16,128]{2,1,0:T(8,128)(2,1)S(1)}, u32[]{:S(2)}, u32[]{:S(2)}) collective-permute-start(bf16[64,16,128]{2,1,0:T(8,128)(2,1)S(1)} %get-tuple-element.34), channel_id=1, source_target_pairs={{0,4},{4,0},{8,12},{12,8},{1,5},{5,1},{9,13},{13,9},{2,6},{6,2},{1... | collective-permute-start | bytes 786440 | tf_op jit(solution)/shard_map/ppermute | solution.py:368
  88.3 13.0 %collective-permute-start.12 = (bf16[64,16,128]{2,1,0:T(8,128)(2,1)S(1)}, bf16[64,16,128]{2,1,0:T(8,128)(2,1)S(1)}, u32[]{:S(2)}, u32[]{:S(2)}) collective-permute-start(bf16[64,16,128]{2,1,0:T(8,128)(2,1)S(1)} %get-tuple-element.35), channel_id=1, source_target_pairs={{0,8},{4,12},{8,0},{12,4},{1,9},{5,13},{9,1},{13,5},{2,10},{6,14},... | collective-permute-start | bytes 786440 | tf_op jit(solution)/shard_map/ppermute | solution.py:368
  90.3 12.5 %collective-permute-start.13 = (bf16[64,16,128]{2,1,0:T(8,128)(2,1)S(1)}, bf16[64,16,128]{2,1,0:T(8,128)(2,1)S(1)}, u32[]{:S(2)}, u32[]{:S(2)}) collective-permute-start(bf16[64,16,128]{2,1,0:T(8,128)(2,1)S(1)} %get-tuple-element.36), channel_id=1, source_target_pairs={{0,12},{4,8},{8,4},{12,0},{1,13},{5,9},{9,5},{13,1},{2,14},{6,10},... | collective-permute-start | bytes 786440 | tf_op jit(solution)/shard_map/ppermute | solution.py:368
  91.9 11.0 %collective-permute-start.27 = (bf16[64,16,128]{2,1,0:T(8,128)(2,1)S(1)}, bf16[64,16,128]{2,1,0:T(8,128)(2,1)S(1)}, u32[]{:S(2)}, u32[]{:S(2)}) collective-permute-start(bf16[64,16,128]{2,1,0:T(8,128)(2,1)S(1)} %get-tuple-element.50), channel_id=1, source_target_pairs={{0,1},{1,0},{2,3},{3,2},{4,5},{5,4},{6,7},{7,6},{8,9},{9,8},{10,11... | collective-permute-start | bytes 786440 | tf_op jit(solution)/shard_map/ppermute | solution.py:368
  92.0 21.4 %collective-permute-start.28 = (bf16[64,16,128]{2,1,0:T(8,128)(2,1)S(1)}, bf16[64,16,128]{2,1,0:T(8,128)(2,1)S(1)}, u32[]{:S(2)}, u32[]{:S(2)}) collective-permute-start(bf16[64,16,128]{2,1,0:T(8,128)(2,1)S(1)} %get-tuple-element.51), channel_id=1, source_target_pairs={{0,2},{1,3},{2,0},{3,1},{4,6},{5,7},{6,4},{7,5},{8,10},{9,11},{10,... | collective-permute-start | bytes 786440 | tf_op jit(solution)/shard_map/ppermute | solution.py:368
  97.5 15.9 %collective-permute-start.29 = (bf16[64,16,128]{2,1,0:T(8,128)(2,1)S(1)}, bf16[64,16,128]{2,1,0:T(8,128)(2,1)S(1)}, u32[]{:S(2)}, u32[]{:S(2)}) collective-permute-start(bf16[64,16,128]{2,1,0:T(8,128)(2,1)S(1)} %get-tuple-element.52), channel_id=1, source_target_pairs={{0,3},{1,2},{2,1},{3,0},{4,7},{5,6},{6,5},{7,4},{8,11},{9,10},{10,... | collective-permute-start | bytes 786440 | tf_op jit(solution)/shard_map/ppermute | solution.py:368
where the time goes:
time: 116 us; the launch traced here: 115 us
  starting transfers between devices  50.2 us (43%)
  waiting for transfers between devices  37.8 us (33%)
  Pallas kernels  23.7 us (20%)
  local copies, waits for them, and re-layouts  1.74 us (2%)
    ppermute x15, waiting for transfers between devices, scatter(): lax.ppermute(sends[k], axis, swaps(size, k))  31.4 us
    ppermute x15, starting transfers between devices, scatter(): lax.ppermute(sends[k], axis, swaps(size, k))  18.9 us
    ppermute x4, starting transfers between devices, local(): lax.ppermute(pay_b, both, [(a, a * size + (a ^ k)) for a in range(size)])  13.2 us
    ppermute x6, starting transfers between devices, spread(): lax.ppermute(own, axis, swaps(size, k))  10.4 us
    pallas_call x2, Pallas kernels, product_two(): pl.pallas_call(functools.partial(product_two_kernel, by_rows, here, block...  7.78 us
    pallas_call x2, Pallas kernels, product_one(): pl.pallas_call(functools.partial(product_one_kernel, by_rows, len(lefts),...  7.18 us
    ppermute x3, starting transfers between devices, local(): lax.ppermute(pay_a, 'gy', [(0, k)])  6.98 us
    ppermute x6, waiting for transfers between devices, spread(): lax.ppermute(own, axis, swaps(size, k))  5.46 us
  transfers between devices with their start and end apart: 30, of which 12 were waited for; matrix products, arithmetic and copies ran while one was open for 2% of the time, Pallas kernels for 15%

commit v1 on v0

--- a/solution.py
+++ b/solution.py
@@ -1,4 +1,5 @@
 import functools
+import math
 
 import jax
 import jax.numpy as jnp
@@ -8,7 +9,7 @@
 from jax.sharding import PartitionSpec as P
 
 WIN = 1
-UNROLL = 32
+UNROLL = 64
 VMEM = pltpu.MemorySpace.VMEM
 SMEM = pltpu.MemorySpace.SMEM
 
@@ -70,6 +71,40 @@
 
 def swaps(size, step):
     return [(i, i ^ step) for i in range(size)]
+
+
+def payload_kernel(tiles_ref, turned_ref, first_ref, second_ref, window_ref, sem):
+    copy = pltpu.make_async_copy(tiles_ref.at[0], window_ref, sem)
+    copy.start()
+    slots, _ = window_ref.shape[:2]
+    height = (first_ref.shape[0] - 16) // slots
+    size = lax.axis_size("gy")
+    rows = height // size
+    tail = jnp.broadcast_to(turned_ref[:, 0:1].astype(jnp.float32), (slots, first_ref.shape[1]))
+    tail = jnp.concatenate([tail, jnp.zeros((16 - slots, first_ref.shape[1]), jnp.float32)], axis=0)
+    tail = tail.astype(jnp.bfloat16)
+    copy.wait()
+    for half, ref in enumerate((first_ref, second_ref)):
+        for k in range(slots):
+            for r in range(size):
+                start = (2 * r + half) * rows
+                ref[k * height + r * rows : k * height + (r + 1) * rows] = window_ref[k, start : start + rows]
+        ref[slots * height :] = tail
+
+
+def payloads(tiles, columns, height):
+    slots, tile = tiles.shape[1:3]
+    shape = jax.ShapeDtypeStruct((slots * height + 16, tile), jnp.bfloat16)
+    return pl.pallas_call(
+        payload_kernel,
+        out_shape=[shape] * 2,
+        in_specs=[pl.BlockSpec(memory_space=pltpu.HBM), pl.BlockSpec(memory_space=VMEM)],
+        out_specs=[pl.BlockSpec(memory_space=VMEM)] * 2,
+        scratch_shapes=[pltpu.VMEM(tiles.shape[1:], jnp.bfloat16), pltpu.SemaphoreType.DMA],
+        compiler_params=limit(50),
+        cost_estimate=pl.CostEstimate(flops=1_000_000, bytes_accessed=400_000, transcendentals=0),
+        name="payload",
+    )(tiles, columns.T)
 
 
 def invert_kernel(cols_ref, inv_ref):
@@ -123,7 +158,7 @@
 
         @pl.when(chosen == k)
         def _(k=k):
-            left_ref[...] = left_refs[k][...]
+            left_ref[pl.ds(slots * height, 16)] = left_refs[k][pl.ds(slots * height, 16)]
 
     tail = left_ref[pl.ds(slots * height, 16), :].astype(jnp.float32)
     columns = [jnp.max(tail[k : k + 1, :]).astype(jnp.int32) for k in range(slots)]
@@ -152,6 +187,12 @@
                         pltpu.make_async_copy(
                             part_refs[t].at[lax.rem(p, here), j], tile_ref.at[k, n], sems.at[k, n]
                         ).start()
+
+    for k in range(lefts):
+
+        @pl.when(chosen == k)
+        def _(k=k):
+            left_ref[pl.ds(0, slots * height)] = left_refs[k][pl.ds(0, slots * height)]
 
     lane = lax.broadcasted_iota(jnp.int32, (rows, left_ref.shape[1]), 1)
     places = jnp.zeros_like(lane)
@@ -272,9 +313,11 @@
             value = extra * left_ref[m, same].astype(jnp.float32) - 2.0 * summed[m * rows : (m + 1) * rows]
             send_refs[m][q] = value.astype(jnp.bfloat16)
 
-    @pl.loop(0, slab, step=UNROLL)
+    unroll = math.gcd(UNROLL, slab)
+
+    @pl.loop(0, slab, step=unroll)
     def _(first):
-        for u in range(UNROLL):
+        for u in range(unroll):
             q = first + u
             entries = [index_ref[q, n] if by_rows else index_ref[n, q] for n in range(slots)]
             if by_rows:
@@ -338,37 +381,36 @@
 def local(block_values, block_cols):
     tiles_here = block_values[0, :, 0]
     columns_here = block_cols[0, :, 0]
-    here, slots, tile, _ = tiles_here.shape
+    here, _, tile, _ = tiles_here.shape
     parts = lax.axis_size("gx")
     size = lax.axis_size("gy")
     blocks = WIN * tile // size
     rows = blocks // 2
     height = rows * size
 
-    def payload(first):
-        window = tiles_here[0].reshape(slots, size, blocks, tile)[:, :, first : first + rows]
-        tail = jnp.broadcast_to(columns_here[0].astype(jnp.bfloat16)[:, None], (slots, tile))
-        tail = jnp.pad(tail, ((0, 16 - slots), (0, 0)))
-        return jnp.concatenate([window.reshape(slots * height, tile), tail], axis=0)
-
-    pay_a, pay_b = payload(0), payload(rows)
+    pay_a, pay_b = payloads(tiles_here, columns_here, height)
     both = ("gy", "gz")
     shifts = [[((i + t) % parts, i) for i in range(parts)] for t in range(1, parts)]
     others = [lax.ppermute(columns_here, "gx", s) for s in shifts]
     moved = [lax.ppermute(tiles_here, "gx", s) for s in shifts]
-    left_b = [
-        lax.ppermute(pay_b, both, [(a, a * size + (a ^ k)) for a in range(size)]) for k in range(size)
-    ]
-    left_a = [pay_a] + [lax.ppermute(pay_a, "gy", [(0, k)]) for k in range(1, size)]
+    left_b = []
+    for k in range(size):
+        left_b.append(lax.ppermute(pay_b, both, [(a, a * size + (a ^ k)) for a in range(size)]))
+    left_a = [pay_a]
+    for k in range(1, size):
+        left_a.append(lax.ppermute(pay_a, "gy", [(0, k)]))
     columns = jnp.concatenate([columns_here] + others, axis=0)
     inverse = invert(columns)
     pieces = [tiles_here] + moved
 
     def scatter(sends, axis):
-        return [sends[0]] + [lax.ppermute(sends[k], axis, swaps(size, k)) for k in range(1, size)]
+        received = [sends[0]]
+        for k in range(1, size):
+            received.append(lax.ppermute(sends[k], axis, swaps(size, k)))
+        return received
 
     def spread(own, axis):
-        return [own] + [lax.ppermute(own, axis, swaps(size, k)) for k in range(1, size)]
+        return scatter([own] * size, axis)
 
     sends_a = product_one(False, inverse, left_a, pieces, size, height)
     parts_a = scatter(sends_a, "gz")

time: 116 us -> 117 us (level)
  Pallas kernels: 23.7 us -> 24.9 us
  transfers between devices with their start and end apart: 30 -> 30, of which waited for: 12 -> 12; matrix products, arithmetic and copies ran while one was open for 2% -> 1% of each run, Pallas kernels for 15% -> 16%
where the time goes in v1:
time: 117 us; the launch traced here: 115 us
  starting transfers between devices  50.8 us (43%)
  waiting for transfers between devices  38.3 us (33%)
  Pallas kernels  24.9 us (21%)
    ppermute x21, waiting for transfers between devices, scatter(): received.append(lax.ppermute(sends[k], axis, swaps(size, k)))  37.1 us
    ppermute x21, starting transfers between devices, scatter(): received.append(lax.ppermute(sends[k], axis, swaps(size, k)))  29.3 us
    ppermute x4, starting transfers between devices, local(): lax.ppermute(pay_b, both, [(a, a * size + (a ^ k)) for a in range(size)])  13.8 us
    pallas_call x2, Pallas kernels, product_two(): pl.pallas_call(functools.partial(product_two_kernel, by_rows, here, block...  7.97 us
    pallas_call x2, Pallas kernels, product_one(): pl.pallas_call(functools.partial(product_one_kernel, by_rows, len(lefts),...  7.17 us
    ppermute x3, starting transfers between devices, local(): left_a.append(lax.ppermute(pay_a, 'gy', [(0, k)]))  6.98 us
    pallas_call x1, Pallas kernels, assemble(): pl.pallas_call(functools.partial(assemble_kernel, len(parts)), out_shape=...  4.62 us
  transfers between devices with their start and end apart: 30, of which 12 were waited for; matrix products, arithmetic and copies ran while one was open for 1% of the time, Pallas kernels for 16%

profile of v1, /device:TPU:0, one launch (start us, length us, event | category | flops | bytes accessed | tf_op | source)
XLA Modules:
  0.0 115.1 jit_solution(239404909165689300)
XLA Ops:
  0.0 0.5 collective-permute-start.1
  0.5 0.7 copy.11
  1.2 1.0 payload.1
  2.1 4.4 %collective-permute-start.2 = (bf16[400,128]{1,0:T(8,128)(2,1)S(1)}, bf16[400,128]{1,0:T(8,128)(2,1)S(1)}, u32[]{:S(2)}, u32[]{:S(2)}) collective-permute-start(bf16[400,128]{1,0:T(8,128)(2,1)S(1)} %get-tuple-element.31.refs_0_), channel_id=1, source_target_pairs={{0,4},{1,5},{2,6},{3,7},{16,20},{17,21},{18,22},{19,23}} | collective-permute-start | bytes 307208 | tf_op jit(solution)/shard_map/ppermute | solution.py:401
  6.5 1.3 %collective-permute-start.3 = (bf16[400,128]{1,0:T(8,128)(2,1)S(1)}, bf16[400,128]{1,0:T(8,128)(2,1)S(1)}, u32[]{:S(2)}, u32[]{:S(2)}) collective-permute-start(bf16[400,128]{1,0:T(8,128)(2,1)S(1)} %get-tuple-element.31.refs_0_), channel_id=1, source_target_pairs={{0,8},{1,9},{2,10},{3,11},{16,24},{17,25},{18,26},{19,27}} | collective-permute-start | bytes 307208 | tf_op jit(solution)/shard_map/ppermute | solution.py:401
  7.8 1.3 %collective-permute-start.4 = (bf16[400,128]{1,0:T(8,128)(2,1)S(1)}, bf16[400,128]{1,0:T(8,128)(2,1)S(1)}, u32[]{:S(2)}, u32[]{:S(2)}) collective-permute-start(bf16[400,128]{1,0:T(8,128)(2,1)S(1)} %get-tuple-element.31.refs_0_), channel_id=1, source_target_pairs={{0,12},{1,13},{2,14},{3,15},{16,28},{17,29},{18,30},{19,31}} | collective-permute-start | bytes 307208 | tf_op jit(solution)/shard_map/ppermute | solution.py:401
  9.1 0.3 collective-permute-start
  9.4 1.2 %collective-permute-done = s32[32,6]{0,1:T(8,128)S(1)} collective-permute-done((s32[32,6]{0,1:T(8,128)S(1)}, s32[32,6]{0,1:T(8,128)S(1)}, u32[]{:S(2)}, u32[]{:S(2)}) %collective-permute-start) | collective-permute-done | bytes 800 | tf_op jit(solution)/shard_map/ppermute | solution.py:394
  10.6 0.7 collective-permute-start.14
  11.3 7.6 %collective-permute-start.15 = (bf16[400,128]{1,0:T(8,128)(2,1)S(1)}, bf16[400,128]{1,0:T(8,128)(2,1)S(1)}, u32[]{:S(2)}, u32[]{:S(2)}) collective-permute-start(bf16[400,128]{1,0:T(8,128)(2,1)S(1)} %get-tuple-element.40), channel_id=1, source_target_pairs={{0,1},{1,4},{2,11},{3,14},{16,17},{17,20},{18,27},{19,30}} | collective-permute-start | bytes 307208 | tf_op jit(solution)/shard_map/ppermute | solution.py:398
  18.9 2.7 %collective-permute-start.16 = (bf16[400,128]{1,0:T(8,128)(2,1)S(1)}, bf16[400,128]{1,0:T(8,128)(2,1)S(1)}, u32[]{:S(2)}, u32[]{:S(2)}) collective-permute-start(bf16[400,128]{1,0:T(8,128)(2,1)S(1)} %get-tuple-element.40), channel_id=1, source_target_pairs={{0,2},{1,7},{2,8},{3,13},{16,18},{17,23},{18,24},{19,29}} | collective-permute-start | bytes 307208 | tf_op jit(solution)/shard_map/ppermute | solution.py:398
  21.6 2.9 %collective-permute-start.17 = (bf16[400,128]{1,0:T(8,128)(2,1)S(1)}, bf16[400,128]{1,0:T(8,128)(2,1)S(1)}, u32[]{:S(2)}, u32[]{:S(2)}) collective-permute-start(bf16[400,128]{1,0:T(8,128)(2,1)S(1)} %get-tuple-element.40), channel_id=1, source_target_pairs={{0,3},{1,6},{2,9},{3,12},{16,19},{17,22},{18,25},{19,28}} | collective-permute-start | bytes 307208 | tf_op jit(solution)/shard_map/ppermute | solution.py:398
  24.7 0.4 invert.1.index_ref
  25.1 3.5 %one_columns.1 = (bf16[37,16,128]{2,1,0:T(8,128)(2,1)S(1)}, bf16[37,16,128]{2,1,0:T(8,128)(2,1)S(1)}, bf16[37,16,128]{2,1,0:T(8,128)(2,1)S(1)}, bf16[37,16,128]{2,1,0:T(8,128)(2,1)S(1)}) custom-call(s32[8,128]{1,0:T(8,128)S(1)} %invert.1.index_ref, bf16[400,128]{1,0:T(8,128)(2,1)S(1)} %get-tuple-element.31.refs_0_, ...), custom_call_target="tpu_custom_call" | custom-call | flops 12000000 | bytes 4000000 | tf_op jit(solution)/shard_map/one_columns/pallas_call | solution.py:227
  28.6 3.7 %one_rows.1 = (bf16[37,16,128]{2,1,0:T(8,128)(2,1)S(1)}, bf16[37,16,128]{2,1,0:T(8,128)(2,1)S(1)}, bf16[37,16,128]{2,1,0:T(8,128)(2,1)S(1)}, bf16[37,16,128]{2,1,0:T(8,128)(2,1)S(1)}) custom-call(s32[64,6]{1,0:T(8,128)S(1)} %copy.5.cols_ref.index_ref, bf16[400,128]{1,0:T(8,128)(2,1)S(1)} %collective-permute-done.14.refs_0_, ...), custom_call_target="tpu_custom_call" | custom-call | flops 12000000 | bytes 4000000 | tf_op jit(solution)/shard_map/one_rows/pallas_call | solution.py:227
  32.4 2.9 %collective-permute-start.19 = (bf16[37,16,128]{2,1,0:T(8,128)(2,1)S(1)}, bf16[37,16,128]{2,1,0:T(8,128)(2,1)S(1)}, u32[]{:S(2)}, u32[]{:S(2)}) collective-permute-start(bf16[37,16,128]{2,1,0:T(8,128)(2,1)S(1)} %get-tuple-element.47), channel_id=1, source_target_pairs={{0,8},{4,12},{8,0},{12,4},{1,9},{5,13},{9,1},{13,5},{2,10},{6,14},... | collective-permute-start | bytes 454664 | tf_op jit(solution)/shard_map/ppermute | solution.py:409
  35.3 1.1 collective-permute-start.20
  36.4 2.8 %collective-permute-done.18.refs_1_ = bf16[37,16,128]{2,1,0:T(8,128)(2,1)S(1)} collective-permute-done((bf16[37,16,128]{2,1,0:T(8,128)(2,1)S(1)}, bf16[37,16,128]{2,1,0:T(8,128)(2,1)S(1)}, u32[]{:S(2)}, u32[]{:S(2)}) %collective-permute-start.18) | collective-permute-done | bytes 151584 | tf_op jit(solution)/shard_map/ppermute | solution.py:409
  39.2 1.7 %collective-permute-done.19.refs_2_ = bf16[37,16,128]{2,1,0:T(8,128)(2,1)S(1)} collective-permute-done((bf16[37,16,128]{2,1,0:T(8,128)(2,1)S(1)}, bf16[37,16,128]{2,1,0:T(8,128)(2,1)S(1)}, u32[]{:S(2)}, u32[]{:S(2)}) %collective-permute-start.19) | collective-permute-done | bytes 151584 | tf_op jit(solution)/shard_map/ppermute | solution.py:409
  40.9 1.5 %collective-permute-done.20.refs_3_ = bf16[37,16,128]{2,1,0:T(8,128)(2,1)S(1)} collective-permute-done((bf16[37,16,128]{2,1,0:T(8,128)(2,1)S(1)}, bf16[37,16,128]{2,1,0:T(8,128)(2,1)S(1)}, u32[]{:S(2)}, u32[]{:S(2)}) %collective-permute-start.20) | collective-permute-done | bytes 151584 | tf_op jit(solution)/shard_map/ppermute | solution.py:409
  42.3 1.1 merge.3.refs_0_
  43.5 0.9 collective-permute-start.21
  44.4 2.1 %collective-permute-start.5 = (bf16[37,16,128]{2,1,0:T(8,128)(2,1)S(1)}, bf16[37,16,128]{2,1,0:T(8,128)(2,1)S(1)}, u32[]{:S(2)}, u32[]{:S(2)}) collective-permute-start(bf16[37,16,128]{2,1,0:T(8,128)(2,1)S(1)} %get-tuple-element.33), channel_id=1, source_target_pairs={{0,1},{1,0},{2,3},{3,2},{4,5},{5,4},{6,7},{7,6},{8,9},{9,8},{10,11... | collective-permute-start | bytes 454664 | tf_op jit(solution)/shard_map/ppermute | solution.py:409
  46.5 2.4 %collective-permute-start.7 = (bf16[37,16,128]{2,1,0:T(8,128)(2,1)S(1)}, bf16[37,16,128]{2,1,0:T(8,128)(2,1)S(1)}, u32[]{:S(2)}, u32[]{:S(2)}) collective-permute-start(bf16[37,16,128]{2,1,0:T(8,128)(2,1)S(1)} %get-tuple-element.35), channel_id=1, source_target_pairs={{0,3},{1,2},{2,1},{3,0},{4,7},{5,6},{6,5},{7,4},{8,11},{9,10},{10,... | collective-permute-start | bytes 454664 | tf_op jit(solution)/shard_map/ppermute | solution.py:409
  48.8 1.7 %collective-permute-start.22 = (bf16[64,16,128]{2,1,0:T(8,128)(2,1)S(1)}, bf16[64,16,128]{2,1,0:T(8,128)(2,1)S(1)}, u32[]{:S(2)}, u32[]{:S(2)}) collective-permute-start(bf16[64,16,128]{2,1,0:T(8,128)(2,1)S(1)} %merge.3.refs_0_), channel_id=1, source_target_pairs={{0,8},{4,12},{8,0},{12,4},{1,9},{5,13},{9,1},{13,5},{2,10},{6,14},... | collective-permute-start | bytes 786440 | tf_op jit(solution)/shard_map/ppermute | solution.py:409
  50.5 0.4 collective-permute-done.5.refs_1_
  51.0 1.3 %collective-permute-start.23 = (bf16[64,16,128]{2,1,0:T(8,128)(2,1)S(1)}, bf16[64,16,128]{2,1,0:T(8,128)(2,1)S(1)}, u32[]{:S(2)}, u32[]{:S(2)}) collective-permute-start(bf16[64,16,128]{2,1,0:T(8,128)(2,1)S(1)} %merge.3.refs_0_), channel_id=1, source_target_pairs={{0,12},{4,8},{8,4},{12,0},{1,13},{5,9},{9,5},{13,1},{2,14},{6,10},... | collective-permute-start | bytes 786440 | tf_op jit(solution)/shard_map/ppermute | solution.py:409
  52.3 6.8 %collective-permute-done.6.refs_2_ = bf16[37,16,128]{2,1,0:T(8,128)(2,1)S(1)} collective-permute-done((bf16[37,16,128]{2,1,0:T(8,128)(2,1)S(1)}, bf16[37,16,128]{2,1,0:T(8,128)(2,1)S(1)}, u32[]{:S(2)}, u32[]{:S(2)}) %collective-permute-start.6) | collective-permute-done | bytes 151584 | tf_op jit(solution)/shard_map/ppermute | solution.py:409
  59.1 1.1 merge.2.refs_0_
  60.2 1.4 %collective-permute-start.10 = (bf16[64,16,128]{2,1,0:T(8,128)(2,1)S(1)}, bf16[64,16,128]{2,1,0:T(8,128)(2,1)S(1)}, u32[]{:S(2)}, u32[]{:S(2)}) collective-permute-start(bf16[64,16,128]{2,1,0:T(8,128)(2,1)S(1)} %merge.2.refs_0_), channel_id=1, source_target_pairs={{0,3},{1,2},{2,1},{3,0},{4,7},{5,6},{6,5},{7,4},{8,11},{9,10},{10,... | collective-permute-start | bytes 786440 | tf_op jit(solution)/shard_map/ppermute | solution.py:409
  61.6 4.7 %collective-permute-start.8 = (bf16[64,16,128]{2,1,0:T(8,128)(2,1)S(1)}, bf16[64,16,128]{2,1,0:T(8,128)(2,1)S(1)}, u32[]{:S(2)}, u32[]{:S(2)}) collective-permute-start(bf16[64,16,128]{2,1,0:T(8,128)(2,1)S(1)} %merge.2.refs_0_), channel_id=1, source_target_pairs={{0,1},{1,0},{2,3},{3,2},{4,5},{5,4},{6,7},{7,6},{8,9},{9,8},{10,11... | collective-permute-start | bytes 786440 | tf_op jit(solution)/shard_map/ppermute | solution.py:409
  66.3 0.5 collective-permute-start.9
  66.8 4.6 %assemble.1.slab_ref = bf16[64,6,128,128]{3,2,1,0:T(8,128)(2,1)S(1)} custom-call(bf16[32,6,128,128]{3,2,1,0:T(8,128)(2,1)} %bitcast.14, bf16[32,6,128,128]{3,2,1,0:T(8,128)(2,1)} %collective-permute-done.1.refs_1_.refs_5_), custom_call_target="tpu_custom_call" | custom-call | flops 4000000 | bytes 25000000 | tf_op jit(solution)/shard_map/assemble/pallas_call | solution.py:37
  71.4 4.7 %two_rows.1 = (bf16[64,16,128]{2,1,0:T(8,128)(2,1)S(1)}, bf16[64,16,128]{2,1,0:T(8,128)(2,1)S(1)}, bf16[64,16,128]{2,1,0:T(8,128)(2,1)S(1)}, bf16[64,16,128]{2,1,0:T(8,128)(2,1)S(1)}) custom-call(s32[64,6]{1,0:T(8,128)S(1)} %copy.5.cols_ref.index_ref, bf16[64,6,128,128]{3,2,1,0:T(8,128)(2,1)S(1)} %assemble.1.slab_ref, ...), custom_call_target="tpu_custom_call" | custom-call | flops 30000000 | bytes 12000000 | tf_op jit(solution)/shard_map/two_rows/pallas_call | solution.py:337
  76.3 3.4 %collective-permute-start.26 = (bf16[64,16,128]{2,1,0:T(8,128)(2,1)S(1)}, bf16[64,16,128]{2,1,0:T(8,128)(2,1)S(1)}, u32[]{:S(2)}, u32[]{:S(2)}) collective-permute-start(bf16[64,16,128]{2,1,0:T(8,128)(2,1)S(1)} %get-tuple-element.52), channel_id=1, source_target_pairs={{0,12},{4,8},{8,4},{12,0},{1,13},{5,9},{9,5},{13,1},{2,14},{6,10},... | collective-permute-start | bytes 786440 | tf_op jit(solution)/shard_map/ppermute | solution.py:409
  79.7 5.7 %collective-permute-done.9.refs_2_ = bf16[64,16,128]{2,1,0:T(8,128)(2,1)S(1)} collective-permute-done((bf16[64,16,128]{2,1,0:T(8,128)(2,1)S(1)}, bf16[64,16,128]{2,1,0:T(8,128)(2,1)S(1)}, u32[]{:S(2)}, u32[]{:S(2)}) %collective-permute-start.9) | collective-permute-done | bytes 262176 | tf_op jit(solution)/shard_map/ppermute | solution.py:409
  85.3 3.3 %two_columns.1 = (bf16[64,16,128]{2,1,0:T(8,128)(2,1)S(1)}, bf16[64,16,128]{2,1,0:T(8,128)(2,1)S(1)}, bf16[64,16,128]{2,1,0:T(8,128)(2,1)S(1)}, bf16[64,16,128]{2,1,0:T(8,128)(2,1)S(1)}) custom-call(s32[8,128]{1,0:T(8,128)S(1)} %invert.1.index_ref, bf16[64,6,128,128]{3,2,1,0:T(8,128)(2,1)S(1)} %assemble.1.slab_ref, bf16[64,16,128]{2,1,0:T(8,128)(2,1)S(1)} %merge.2.refs_0_, ...), custom_call_target="tpu_custom_call" | custom-call | flops 30000000 | bytes 12000000 | tf_op jit(solution)/shard_map/two_columns/pallas_call | solution.py:337
  88.7 1.9 %collective-permute-start.12 = (bf16[64,16,128]{2,1,0:T(8,128)(2,1)S(1)}, bf16[64,16,128]{2,1,0:T(8,128)(2,1)S(1)}, u32[]{:S(2)}, u32[]{:S(2)}) collective-permute-start(bf16[64,16,128]{2,1,0:T(8,128)(2,1)S(1)} %get-tuple-element.38), channel_id=1, source_target_pairs={{0,8},{4,12},{8,0},{12,4},{1,9},{5,13},{9,1},{13,5},{2,10},{6,14},... | collective-permute-start | bytes 786440 | tf_op jit(solution)/shard_map/ppermute | solution.py:409
  90.6 1.5 %collective-permute-start.13 = (bf16[64,16,128]{2,1,0:T(8,128)(2,1)S(1)}, bf16[64,16,128]{2,1,0:T(8,128)(2,1)S(1)}, u32[]{:S(2)}, u32[]{:S(2)}) collective-permute-start(bf16[64,16,128]{2,1,0:T(8,128)(2,1)S(1)} %get-tuple-element.39), channel_id=1, source_target_pairs={{0,12},{4,8},{8,4},{12,0},{1,13},{5,9},{9,5},{13,1},{2,14},{6,10},... | collective-permute-start | bytes 786440 | tf_op jit(solution)/shard_map/ppermute | solution.py:409
  92.2 0.1 pick.1
  92.4 1.8 %collective-permute-start.28 = (bf16[64,16,128]{2,1,0:T(8,128)(2,1)S(1)}, bf16[64,16,128]{2,1,0:T(8,128)(2,1)S(1)}, u32[]{:S(2)}, u32[]{:S(2)}) collective-permute-start(bf16[64,16,128]{2,1,0:T(8,128)(2,1)S(1)} %get-tuple-element.55), channel_id=1, source_target_pairs={{0,2},{1,3},{2,0},{3,1},{4,6},{5,7},{6,4},{7,5},{8,10},{9,11},{10,... | collective-permute-start | bytes 786440 | tf_op jit(solution)/shard_map/ppermute | solution.py:409
  94.2 3.6 %collective-permute-done.11.refs_1_ = bf16[64,16,128]{2,1,0:T(8,128)(2,1)S(1)} collective-permute-done((bf16[64,16,128]{2,1,0:T(8,128)(2,1)S(1)}, bf16[64,16,128]{2,1,0:T(8,128)(2,1)S(1)}, u32[]{:S(2)}, u32[]{:S(2)}) %collective-permute-start.11) | collective-permute-done | bytes 262176 | tf_op jit(solution)/shard_map/ppermute | solution.py:409
  97.9 1.3 %collective-permute-start.29 = (bf16[64,16,128]{2,1,0:T(8,128)(2,1)S(1)}, bf16[64,16,128]{2,1,0:T(8,128)(2,1)S(1)}, u32[]{:S(2)}, u32[]{:S(2)}) collective-permute-start(bf16[64,16,128]{2,1,0:T(8,128)(2,1)S(1)} %get-tuple-element.56), channel_id=1, source_target_pairs={{0,3},{1,2},{2,1},{3,0},{4,7},{5,6},{6,5},{7,4},{8,11},{9,10},{10,... | collective-permute-start | bytes 786440 | tf_op jit(solution)/shard_map/ppermute | solution.py:409
  99.1 2.5 %collective-permute-done.12.refs_2_ = bf16[64,16,128]{2,1,0:T(8,128)(2,1)S(1)} collective-permute-done((bf16[64,16,128]{2,1,0:T(8,128)(2,1)S(1)}, bf16[64,16,128]{2,1,0:T(8,128)(2,1)S(1)}, u32[]{:S(2)}, u32[]{:S(2)}) %collective-permute-start.12) | collective-permute-done | bytes 262176 | tf_op jit(solution)/shard_map/ppermute | solution.py:409
  101.7 1.4 %collective-permute-done.13.refs_3_ = bf16[64,16,128]{2,1,0:T(8,128)(2,1)S(1)} collective-permute-done((bf16[64,16,128]{2,1,0:T(8,128)(2,1)S(1)}, bf16[64,16,128]{2,1,0:T(8,128)(2,1)S(1)}, u32[]{:S(2)}, u32[]{:S(2)}) %collective-permute-start.13) | collective-permute-done | bytes 262176 | tf_op jit(solution)/shard_map/ppermute | solution.py:409
  103.1 0.2 collective-permute-done.27.refs_5_
  103.3 10.5 %collective-permute-done.28.refs_6_ = bf16[64,16,128]{2,1,0:T(8,128)(2,1)S(1)} collective-permute-done((bf16[64,16,128]{2,1,0:T(8,128)(2,1)S(1)}, bf16[64,16,128]{2,1,0:T(8,128)(2,1)S(1)}, u32[]{:S(2)}, u32[]{:S(2)}) %collective-permute-start.28) | collective-permute-done | bytes 262176 | tf_op jit(solution)/shard_map/ppermute | solution.py:409
  113.8 1.4 %finish.1 = f32[32,8192]{1,0:T(8,128)} custom-call(bf16[64,16,128]{2,1,0:T(8,128)(2,1)S(1)} %get-tuple-element.36.refs_0_, bf16[64,16,128]{2,1,0:T(8,128)(2,1)S(1)} %collective-permute-done.11.refs_1_, bf16[64,16,128]{2,1,0:T(8,128)(2,1)S(1)} %collective-permute-done.12.refs_2_, bf16[64,16,128]{2,1,0:T(8,128)(2,1)S(1)} %collective-permute-done.13.refs_3_, ...), custom_call_target="tpu_custom_call" | custom-call | tf_op jit(solution)/shard_map/finish/pallas_call | solution.py:371
  (26 shorter events, 0.6 us)
Async XLA Ops:
  0.0 25.1 %collective-permute-start.1 = (bf16[32,6,128,128]{3,2,1,0:T(8,128)(2,1)}, bf16[32,6,128,128]{3,2,1,0:T(8,128)(2,1)}, u32[]{:S(2)}, u32[]{:S(2)}) collective-permute-start(bf16[32,6,128,128]{3,2,1,0:T(8,128)(2,1)} %bitcast.10), channel_id=1, source_target_pairs={{16,0},{0,16},{17,1},{1,17},{18,2},{2,18},{19,3},{3,19},{20,4},{4,... | collective-permute-start | bytes 18874376 | tf_op jit(solution)/shard_map/ppermute | solution.py:395
  2.1 9.1 %collective-permute-start.2 = (bf16[400,128]{1,0:T(8,128)(2,1)S(1)}, bf16[400,128]{1,0:T(8,128)(2,1)S(1)}, u32[]{:S(2)}, u32[]{:S(2)}) collective-permute-start(bf16[400,128]{1,0:T(8,128)(2,1)S(1)} %get-tuple-element.31.refs_0_), channel_id=1, source_target_pairs={{0,4},{1,5},{2,6},{3,7},{16,20},{17,21},{18,22},{19,23}} | collective-permute-start | bytes 307208 | tf_op jit(solution)/shard_map/ppermute | solution.py:401
  6.5 12.3 %collective-permute-start.3 = (bf16[400,128]{1,0:T(8,128)(2,1)S(1)}, bf16[400,128]{1,0:T(8,128)(2,1)S(1)}, u32[]{:S(2)}, u32[]{:S(2)}) collective-permute-start(bf16[400,128]{1,0:T(8,128)(2,1)S(1)} %get-tuple-element.31.refs_0_), channel_id=1, source_target_pairs={{0,8},{1,9},{2,10},{3,11},{16,24},{17,25},{18,26},{19,27}} | collective-permute-start | bytes 307208 | tf_op jit(solution)/shard_map/ppermute | solution.py:401
  7.8 13.8 %collective-permute-start.4 = (bf16[400,128]{1,0:T(8,128)(2,1)S(1)}, bf16[400,128]{1,0:T(8,128)(2,1)S(1)}, u32[]{:S(2)}, u32[]{:S(2)}) collective-permute-start(bf16[400,128]{1,0:T(8,128)(2,1)S(1)} %get-tuple-element.31.refs_0_), channel_id=1, source_target_pairs={{0,12},{1,13},{2,14},{3,15},{16,28},{17,29},{18,30},{19,31}} | collective-permute-start | bytes 307208 | tf_op jit(solution)/shard_map/ppermute | solution.py:401
  9.1 1.5 %collective-permute-start = (s32[32,6]{0,1:T(8,128)S(1)}, s32[32,6]{0,1:T(8,128)S(1)}, u32[]{:S(2)}, u32[]{:S(2)}) collective-permute-start(s32[32,6]{0,1:T(8,128)S(1)} %bitcast.8), channel_id=1, source_target_pairs={{16,0},{0,16},{17,1},{1,17},{18,2},{2,18},{19,3},{3,19},{20,4},{4,... | collective-permute-start | bytes 2312 | tf_op jit(solution)/shard_map/ppermute | solution.py:394
  10.6 17.9 %collective-permute-start.14 = (bf16[400,128]{1,0:T(8,128)(2,1)S(1)}, bf16[400,128]{1,0:T(8,128)(2,1)S(1)}, u32[]{:S(2)}, u32[]{:S(2)}) collective-permute-start(bf16[400,128]{1,0:T(8,128)(2,1)S(1)} %get-tuple-element.40), channel_id=1, source_target_pairs={{0,0},{1,5},{2,10},{3,15},{16,16},{17,21},{18,26},{19,31}} | collective-permute-start | bytes 307208 | tf_op jit(solution)/shard_map/ppermute | solution.py:398
  11.3 17.3 %collective-permute-start.15 = (bf16[400,128]{1,0:T(8,128)(2,1)S(1)}, bf16[400,128]{1,0:T(8,128)(2,1)S(1)}, u32[]{:S(2)}, u32[]{:S(2)}) collective-permute-start(bf16[400,128]{1,0:T(8,128)(2,1)S(1)} %get-tuple-element.40), channel_id=1, source_target_pairs={{0,1},{1,4},{2,11},{3,14},{16,17},{17,20},{18,27},{19,30}} | collective-permute-start | bytes 307208 | tf_op jit(solution)/shard_map/ppermute | solution.py:398
  18.9 9.7 %collective-permute-start.16 = (bf16[400,128]{1,0:T(8,128)(2,1)S(1)}, bf16[400,128]{1,0:T(8,128)(2,1)S(1)}, u32[]{:S(2)}, u32[]{:S(2)}) collective-permute-start(bf16[400,128]{1,0:T(8,128)(2,1)S(1)} %get-tuple-element.40), channel_id=1, source_target_pairs={{0,2},{1,7},{2,8},{3,13},{16,18},{17,23},{18,24},{19,29}} | collective-permute-start | bytes 307208 | tf_op jit(solution)/shard_map/ppermute | solution.py:398
  21.6 7.0 %collective-permute-start.17 = (bf16[400,128]{1,0:T(8,128)(2,1)S(1)}, bf16[400,128]{1,0:T(8,128)(2,1)S(1)}, u32[]{:S(2)}, u32[]{:S(2)}) collective-permute-start(bf16[400,128]{1,0:T(8,128)(2,1)S(1)} %get-tuple-element.40), channel_id=1, source_target_pairs={{0,3},{1,6},{2,9},{3,12},{16,19},{17,22},{18,25},{19,28}} | collective-permute-start | bytes 307208 | tf_op jit(solution)/shard_map/ppermute | solution.py:398
  32.3 6.9 %collective-permute-start.18 = (bf16[37,16,128]{2,1,0:T(8,128)(2,1)S(1)}, bf16[37,16,128]{2,1,0:T(8,128)(2,1)S(1)}, u32[]{:S(2)}, u32[]{:S(2)}) collective-permute-start(bf16[37,16,128]{2,1,0:T(8,128)(2,1)S(1)} %get-tuple-element.46), channel_id=1, source_target_pairs={{0,4},{4,0},{8,12},{12,8},{1,5},{5,1},{9,13},{13,9},{2,6},{6,2},{1... | collective-permute-start | bytes 454664 | tf_op jit(solution)/shard_map/ppermute | solution.py:409
  32.4 8.5 %collective-permute-start.19 = (bf16[37,16,128]{2,1,0:T(8,128)(2,1)S(1)}, bf16[37,16,128]{2,1,0:T(8,128)(2,1)S(1)}, u32[]{:S(2)}, u32[]{:S(2)}) collective-permute-start(bf16[37,16,128]{2,1,0:T(8,128)(2,1)S(1)} %get-tuple-element.47), channel_id=1, source_target_pairs={{0,8},{4,12},{8,0},{12,4},{1,9},{5,13},{9,1},{13,5},{2,10},{6,14},... | collective-permute-start | bytes 454664 | tf_op jit(solution)/shard_map/ppermute | solution.py:409
  35.3 7.0 %collective-permute-start.20 = (bf16[37,16,128]{2,1,0:T(8,128)(2,1)S(1)}, bf16[37,16,128]{2,1,0:T(8,128)(2,1)S(1)}, u32[]{:S(2)}, u32[]{:S(2)}) collective-permute-start(bf16[37,16,128]{2,1,0:T(8,128)(2,1)S(1)} %get-tuple-element.48), channel_id=1, source_target_pairs={{0,12},{4,8},{8,4},{12,0},{1,13},{5,9},{9,5},{13,1},{2,14},{6,10},... | collective-permute-start | bytes 454664 | tf_op jit(solution)/shard_map/ppermute | solution.py:409
  43.5 22.8 %collective-permute-start.21 = (bf16[64,16,128]{2,1,0:T(8,128)(2,1)S(1)}, bf16[64,16,128]{2,1,0:T(8,128)(2,1)S(1)}, u32[]{:S(2)}, u32[]{:S(2)}) collective-permute-start(bf16[64,16,128]{2,1,0:T(8,128)(2,1)S(1)} %merge.3.refs_0_), channel_id=1, source_target_pairs={{0,4},{4,0},{8,12},{12,8},{1,5},{5,1},{9,13},{13,9},{2,6},{6,2},{1... | collective-permute-start | bytes 786440 | tf_op jit(solution)/shard_map/ppermute | solution.py:409
  44.4 6.6 %collective-permute-start.5 = (bf16[37,16,128]{2,1,0:T(8,128)(2,1)S(1)}, bf16[37,16,128]{2,1,0:T(8,128)(2,1)S(1)}, u32[]{:S(2)}, u32[]{:S(2)}) collective-permute-start(bf16[37,16,128]{2,1,0:T(8,128)(2,1)S(1)} %get-tuple-element.33), channel_id=1, source_target_pairs={{0,1},{1,0},{2,3},{3,2},{4,5},{5,4},{6,7},{7,6},{8,9},{9,8},{10,11... | collective-permute-start | bytes 454664 | tf_op jit(solution)/shard_map/ppermute | solution.py:409
  46.5 12.6 %collective-permute-start.6 = (bf16[37,16,128]{2,1,0:T(8,128)(2,1)S(1)}, bf16[37,16,128]{2,1,0:T(8,128)(2,1)S(1)}, u32[]{:S(2)}, u32[]{:S(2)}) collective-permute-start(bf16[37,16,128]{2,1,0:T(8,128)(2,1)S(1)} %get-tuple-element.34), channel_id=1, source_target_pairs={{0,2},{1,3},{2,0},{3,1},{4,6},{5,7},{6,4},{7,5},{8,10},{9,11},{10,... | collective-permute-start | bytes 454664 | tf_op jit(solution)/shard_map/ppermute | solution.py:409
  46.5 12.6 %collective-permute-start.7 = (bf16[37,16,128]{2,1,0:T(8,128)(2,1)S(1)}, bf16[37,16,128]{2,1,0:T(8,128)(2,1)S(1)}, u32[]{:S(2)}, u32[]{:S(2)}) collective-permute-start(bf16[37,16,128]{2,1,0:T(8,128)(2,1)S(1)} %get-tuple-element.35), channel_id=1, source_target_pairs={{0,3},{1,2},{2,1},{3,0},{4,7},{5,6},{6,5},{7,4},{8,11},{9,10},{10,... | collective-permute-start | bytes 454664 | tf_op jit(solution)/shard_map/ppermute | solution.py:409
  48.8 22.6 %collective-permute-start.22 = (bf16[64,16,128]{2,1,0:T(8,128)(2,1)S(1)}, bf16[64,16,128]{2,1,0:T(8,128)(2,1)S(1)}, u32[]{:S(2)}, u32[]{:S(2)}) collective-permute-start(bf16[64,16,128]{2,1,0:T(8,128)(2,1)S(1)} %merge.3.refs_0_), channel_id=1, source_target_pairs={{0,8},{4,12},{8,0},{12,4},{1,9},{5,13},{9,1},{13,5},{2,10},{6,14},... | collective-permute-start | bytes 786440 | tf_op jit(solution)/shard_map/ppermute | solution.py:409
  51.0 20.4 %collective-permute-start.23 = (bf16[64,16,128]{2,1,0:T(8,128)(2,1)S(1)}, bf16[64,16,128]{2,1,0:T(8,128)(2,1)S(1)}, u32[]{:S(2)}, u32[]{:S(2)}) collective-permute-start(bf16[64,16,128]{2,1,0:T(8,128)(2,1)S(1)} %merge.3.refs_0_), channel_id=1, source_target_pairs={{0,12},{4,8},{8,4},{12,0},{1,13},{5,9},{9,5},{13,1},{2,14},{6,10},... | collective-permute-start | bytes 786440 | tf_op jit(solution)/shard_map/ppermute | solution.py:409
  60.2 16.0 %collective-permute-start.10 = (bf16[64,16,128]{2,1,0:T(8,128)(2,1)S(1)}, bf16[64,16,128]{2,1,0:T(8,128)(2,1)S(1)}, u32[]{:S(2)}, u32[]{:S(2)}) collective-permute-start(bf16[64,16,128]{2,1,0:T(8,128)(2,1)S(1)} %merge.2.refs_0_), channel_id=1, source_target_pairs={{0,3},{1,2},{2,1},{3,0},{4,7},{5,6},{6,5},{7,4},{8,11},{9,10},{10,... | collective-permute-start | bytes 786440 | tf_op jit(solution)/shard_map/ppermute | solution.py:409
  61.6 18.0 %collective-permute-start.8 = (bf16[64,16,128]{2,1,0:T(8,128)(2,1)S(1)}, bf16[64,16,128]{2,1,0:T(8,128)(2,1)S(1)}, u32[]{:S(2)}, u32[]{:S(2)}) collective-permute-start(bf16[64,16,128]{2,1,0:T(8,128)(2,1)S(1)} %merge.2.refs_0_), channel_id=1, source_target_pairs={{0,1},{1,0},{2,3},{3,2},{4,5},{5,4},{6,7},{7,6},{8,9},{9,8},{10,11... | collective-permute-start | bytes 786440 | tf_op jit(solution)/shard_map/ppermute | solution.py:409
  66.3 19.0 %collective-permute-start.9 = (bf16[64,16,128]{2,1,0:T(8,128)(2,1)S(1)}, bf16[64,16,128]{2,1,0:T(8,128)(2,1)S(1)}, u32[]{:S(2)}, u32[]{:S(2)}) collective-permute-start(bf16[64,16,128]{2,1,0:T(8,128)(2,1)S(1)} %merge.2.refs_0_), channel_id=1, source_target_pairs={{0,2},{1,3},{2,0},{3,1},{4,6},{5,7},{6,4},{7,5},{8,10},{9,11},{10,... | collective-permute-start | bytes 786440 | tf_op jit(solution)/shard_map/ppermute | solution.py:409
  76.1 14.5 %collective-permute-start.24 = (bf16[64,16,128]{2,1,0:T(8,128)(2,1)S(1)}, bf16[64,16,128]{2,1,0:T(8,128)(2,1)S(1)}, u32[]{:S(2)}, u32[]{:S(2)}) collective-permute-start(bf16[64,16,128]{2,1,0:T(8,128)(2,1)S(1)} %get-tuple-element.50), channel_id=1, source_target_pairs={{0,4},{4,0},{8,12},{12,8},{1,5},{5,1},{9,13},{13,9},{2,6},{6,2},{1... | collective-permute-start | bytes 786440 | tf_op jit(solution)/shard_map/ppermute | solution.py:409
  76.2 16.0 %collective-permute-start.25 = (bf16[64,16,128]{2,1,0:T(8,128)(2,1)S(1)}, bf16[64,16,128]{2,1,0:T(8,128)(2,1)S(1)}, u32[]{:S(2)}, u32[]{:S(2)}) collective-permute-start(bf16[64,16,128]{2,1,0:T(8,128)(2,1)S(1)} %get-tuple-element.51), channel_id=1, source_target_pairs={{0,8},{4,12},{8,0},{12,4},{1,9},{5,13},{9,1},{13,5},{2,10},{6,14},... | collective-permute-start | bytes 786440 | tf_op jit(solution)/shard_map/ppermute | solution.py:409
  76.3 15.9 %collective-permute-start.26 = (bf16[64,16,128]{2,1,0:T(8,128)(2,1)S(1)}, bf16[64,16,128]{2,1,0:T(8,128)(2,1)S(1)}, u32[]{:S(2)}, u32[]{:S(2)}) collective-permute-start(bf16[64,16,128]{2,1,0:T(8,128)(2,1)S(1)} %get-tuple-element.52), channel_id=1, source_target_pairs={{0,12},{4,8},{8,4},{12,0},{1,13},{5,9},{9,5},{13,1},{2,14},{6,10},... | collective-permute-start | bytes 786440 | tf_op jit(solution)/shard_map/ppermute | solution.py:409
  88.6 9.2 %collective-permute-start.11 = (bf16[64,16,128]{2,1,0:T(8,128)(2,1)S(1)}, bf16[64,16,128]{2,1,0:T(8,128)(2,1)S(1)}, u32[]{:S(2)}, u32[]{:S(2)}) collective-permute-start(bf16[64,16,128]{2,1,0:T(8,128)(2,1)S(1)} %get-tuple-element.37), channel_id=1, source_target_pairs={{0,4},{4,0},{8,12},{12,8},{1,5},{5,1},{9,13},{13,9},{2,6},{6,2},{1... | collective-permute-start | bytes 786440 | tf_op jit(solution)/shard_map/ppermute | solution.py:409
  88.7 13.0 %collective-permute-start.12 = (bf16[64,16,128]{2,1,0:T(8,128)(2,1)S(1)}, bf16[64,16,128]{2,1,0:T(8,128)(2,1)S(1)}, u32[]{:S(2)}, u32[]{:S(2)}) collective-permute-start(bf16[64,16,128]{2,1,0:T(8,128)(2,1)S(1)} %get-tuple-element.38), channel_id=1, source_target_pairs={{0,8},{4,12},{8,0},{12,4},{1,9},{5,13},{9,1},{13,5},{2,10},{6,14},... | collective-permute-start | bytes 786440 | tf_op jit(solution)/shard_map/ppermute | solution.py:409
  90.6 12.5 %collective-permute-start.13 = (bf16[64,16,128]{2,1,0:T(8,128)(2,1)S(1)}, bf16[64,16,128]{2,1,0:T(8,128)(2,1)S(1)}, u32[]{:S(2)}, u32[]{:S(2)}) collective-permute-start(bf16[64,16,128]{2,1,0:T(8,128)(2,1)S(1)} %get-tuple-element.39), channel_id=1, source_target_pairs={{0,12},{4,8},{8,4},{12,0},{1,13},{5,9},{9,5},{13,1},{2,14},{6,10},... | collective-permute-start | bytes 786440 | tf_op jit(solution)/shard_map/ppermute | solution.py:409
  92.3 11.0 %collective-permute-start.27 = (bf16[64,16,128]{2,1,0:T(8,128)(2,1)S(1)}, bf16[64,16,128]{2,1,0:T(8,128)(2,1)S(1)}, u32[]{:S(2)}, u32[]{:S(2)}) collective-permute-start(bf16[64,16,128]{2,1,0:T(8,128)(2,1)S(1)} %get-tuple-element.54), channel_id=1, source_target_pairs={{0,1},{1,0},{2,3},{3,2},{4,5},{5,4},{6,7},{7,6},{8,9},{9,8},{10,11... | collective-permute-start | bytes 786440 | tf_op jit(solution)/shard_map/ppermute | solution.py:409
  92.4 21.4 %collective-permute-start.28 = (bf16[64,16,128]{2,1,0:T(8,128)(2,1)S(1)}, bf16[64,16,128]{2,1,0:T(8,128)(2,1)S(1)}, u32[]{:S(2)}, u32[]{:S(2)}) collective-permute-start(bf16[64,16,128]{2,1,0:T(8,128)(2,1)S(1)} %get-tuple-element.55), channel_id=1, source_target_pairs={{0,2},{1,3},{2,0},{3,1},{4,6},{5,7},{6,4},{7,5},{8,10},{9,11},{10,... | collective-permute-start | bytes 786440 | tf_op jit(solution)/shard_map/ppermute | solution.py:409
  97.9 15.9 %collective-permute-start.29 = (bf16[64,16,128]{2,1,0:T(8,128)(2,1)S(1)}, bf16[64,16,128]{2,1,0:T(8,128)(2,1)S(1)}, u32[]{:S(2)}, u32[]{:S(2)}) collective-permute-start(bf16[64,16,128]{2,1,0:T(8,128)(2,1)S(1)} %get-tuple-element.56), channel_id=1, source_target_pairs={{0,3},{1,2},{2,1},{3,0},{4,7},{5,6},{6,5},{7,4},{8,11},{9,10},{10,... | collective-permute-start | bytes 786440 | tf_op jit(solution)/shard_map/ppermute | solution.py:409

commit v2 on v1

--- a/solution.py
+++ b/solution.py
@@ -347,35 +347,40 @@
     )(index, tiles, *rounded)
 
 
-def finish_kernel(here, *refs):
-    half = len(refs) // 2
-    first, second, out_ref = refs[:half], refs[half:-1], refs[-1]
-    g = lax.axis_index("gx")
-    slab, rows, tile = first[0].shape
-
-    def add(refs_in, y):
-        total = refs_in[0][y].astype(jnp.float32)
-        for ref in refs_in[1:]:
-            total = total + ref[y].astype(jnp.float32)
-        return total
+def finish_kernel(here, half, *refs):
+    out_ref, sum_ref, sem = refs[-3:]
+    parts = refs[half:-3]
+    slab, rows, tile = parts[0].shape
+    turn = here * lax.axis_index("gx") if half else 0
 
     @pl.loop(0, slab, unroll=8)
     def _(y):
-        columns = pl.ds(pl.multiple_of(y * tile, tile), tile)
-        out_ref[0:rows, columns] = add(first, y)
-        out_ref[rows : 2 * rows, columns] = add(second, lax.rem(y + slab - here * g, slab))
-
-
-def finish(first, second, here):
-    slab, rows, tile = first[0].shape
-    return pl.pallas_call(
-        functools.partial(finish_kernel, here),
+        q = lax.rem(y + slab - turn, slab) if half else y
+        summed = parts[0][q].astype(jnp.float32)
+        for ref in parts[1:]:
+            summed = summed + ref[q].astype(jnp.float32)
+        sum_ref[:, pl.ds(pl.multiple_of(y * tile, tile), tile)] = summed
+
+    copy = pltpu.make_async_copy(sum_ref, out_ref.at[pl.ds(half * rows, rows)], sem)
+    copy.start()
+    copy.wait()
+
+
+def finish(parts, here, before=None):
+    slab, rows, tile = parts[0].shape
+    ahead = () if before is None else (before,)
+    return pl.pallas_call(
+        functools.partial(finish_kernel, here, len(ahead)),
         out_shape=jax.ShapeDtypeStruct((2 * rows, slab * tile), jnp.float32),
-        in_specs=[pl.BlockSpec(memory_space=VMEM)] * (len(first) + len(second)),
-        out_specs=pl.BlockSpec(memory_space=VMEM),
-        compiler_params=limit(8),
+        in_specs=[pl.BlockSpec(memory_space=pltpu.HBM)] * len(ahead)
+        + [pl.BlockSpec(memory_space=VMEM)] * len(parts),
+        out_specs=pl.BlockSpec(memory_space=pltpu.HBM),
+        scratch_shapes=[pltpu.VMEM((rows, slab * tile), jnp.float32), pltpu.SemaphoreType.DMA],
+        input_output_aliases={0: 0} if ahead else {},
+        compiler_params=limit(50),
+        cost_estimate=pl.CostEstimate(flops=1_000_000, bytes_accessed=1_000_000, transcendentals=0),
         name="finish",
-    )(*first, *second)
+    )(*ahead, *parts)
 
 
 def local(block_values, block_cols):
@@ -428,7 +433,8 @@
     got_b = scatter(picked, "gz")
     out_a = product_two(False, inverse, rounded_a, tiles, here)
     got_a = scatter(out_a, "gy")
-    return finish(got_a, got_b, here)
+    begun = finish(got_a, here)
+    return finish(got_b, here, begun)
 
 
 def solution(mesh):

time: 117 us -> 116 us (level)
  transfers between devices with their start and end apart: 30 -> 30, of which waited for: 12 -> 11; matrix products, arithmetic and copies ran while one was open for 1% -> 1% of each run, Pallas kernels for 16% -> 17%
where the time goes in v2:
time: 116 us; the launch traced here: 115 us
  starting transfers between devices  50.8 us (44%)
  waiting for transfers between devices  37.3 us (32%)
  Pallas kernels  25.6 us (22%)
    ppermute x21, waiting for transfers between devices, scatter(): received.append(lax.ppermute(sends[k], axis, swaps(size, k)))  36.1 us
    ppermute x21, starting transfers between devices, scatter(): received.append(lax.ppermute(sends[k], axis, swaps(size, k)))  29.3 us
    ppermute x4, starting transfers between devices, local(): lax.ppermute(pay_b, both, [(a, a * size + (a ^ k)) for a in range(size)])  13.8 us
    pallas_call x2, Pallas kernels, product_two(): pl.pallas_call(functools.partial(product_two_kernel, by_rows, here, block...  7.97 us
    pallas_call x2, Pallas kernels, product_one(): pl.pallas_call(functools.partial(product_one_kernel, by_rows, len(lefts),...  7.17 us
    ppermute x3, starting transfers between devices, local(): left_a.append(lax.ppermute(pay_a, 'gy', [(0, k)]))  6.98 us
    pallas_call x1, Pallas kernels, assemble(): pl.pallas_call(functools.partial(assemble_kernel, len(parts)), out_shape=...  4.62 us
  transfers between devices with their start and end apart: 30, of which 11 were waited for; matrix products, arithmetic and copies ran while one was open for 1% of the time, Pallas kernels for 17%

profile of v2, /device:TPU:0, one launch (start us, length us, event | category | flops | bytes accessed | tf_op | source)
XLA Modules:
  0.0 114.9 jit_solution(15617916810072384925)
XLA Ops:
  0.0 0.5 collective-permute-start.1
  0.5 0.7 copy.12
  1.2 1.0 payload.1
  2.1 4.4 %collective-permute-start.2 = (bf16[400,128]{1,0:T(8,128)(2,1)S(1)}, bf16[400,128]{1,0:T(8,128)(2,1)S(1)}, u32[]{:S(2)}, u32[]{:S(2)}) collective-permute-start(bf16[400,128]{1,0:T(8,128)(2,1)S(1)} %get-tuple-element.31.refs_0_), channel_id=1, source_target_pairs={{0,4},{1,5},{2,6},{3,7},{16,20},{17,21},{18,22},{19,23}} | collective-permute-start | bytes 307208 | tf_op jit(solution)/shard_map/ppermute | solution.py:406
  6.5 1.3 %collective-permute-start.3 = (bf16[400,128]{1,0:T(8,128)(2,1)S(1)}, bf16[400,128]{1,0:T(8,128)(2,1)S(1)}, u32[]{:S(2)}, u32[]{:S(2)}) collective-permute-start(bf16[400,128]{1,0:T(8,128)(2,1)S(1)} %get-tuple-element.31.refs_0_), channel_id=1, source_target_pairs={{0,8},{1,9},{2,10},{3,11},{16,24},{17,25},{18,26},{19,27}} | collective-permute-start | bytes 307208 | tf_op jit(solution)/shard_map/ppermute | solution.py:406
  7.8 1.3 %collective-permute-start.4 = (bf16[400,128]{1,0:T(8,128)(2,1)S(1)}, bf16[400,128]{1,0:T(8,128)(2,1)S(1)}, u32[]{:S(2)}, u32[]{:S(2)}) collective-permute-start(bf16[400,128]{1,0:T(8,128)(2,1)S(1)} %get-tuple-element.31.refs_0_), channel_id=1, source_target_pairs={{0,12},{1,13},{2,14},{3,15},{16,28},{17,29},{18,30},{19,31}} | collective-permute-start | bytes 307208 | tf_op jit(solution)/shard_map/ppermute | solution.py:406
  9.1 0.3 collective-permute-start
  9.4 1.2 %collective-permute-done = s32[32,6]{0,1:T(8,128)S(1)} collective-permute-done((s32[32,6]{0,1:T(8,128)S(1)}, s32[32,6]{0,1:T(8,128)S(1)}, u32[]{:S(2)}, u32[]{:S(2)}) %collective-permute-start) | collective-permute-done | bytes 800 | tf_op jit(solution)/shard_map/ppermute | solution.py:399
  10.6 0.7 collective-permute-start.14
  11.3 7.6 %collective-permute-start.15 = (bf16[400,128]{1,0:T(8,128)(2,1)S(1)}, bf16[400,128]{1,0:T(8,128)(2,1)S(1)}, u32[]{:S(2)}, u32[]{:S(2)}) collective-permute-start(bf16[400,128]{1,0:T(8,128)(2,1)S(1)} %get-tuple-element.40), channel_id=1, source_target_pairs={{0,1},{1,4},{2,11},{3,14},{16,17},{17,20},{18,27},{19,30}} | collective-permute-start | bytes 307208 | tf_op jit(solution)/shard_map/ppermute | solution.py:403
  18.9 2.7 %collective-permute-start.16 = (bf16[400,128]{1,0:T(8,128)(2,1)S(1)}, bf16[400,128]{1,0:T(8,128)(2,1)S(1)}, u32[]{:S(2)}, u32[]{:S(2)}) collective-permute-start(bf16[400,128]{1,0:T(8,128)(2,1)S(1)} %get-tuple-element.40), channel_id=1, source_target_pairs={{0,2},{1,7},{2,8},{3,13},{16,18},{17,23},{18,24},{19,29}} | collective-permute-start | bytes 307208 | tf_op jit(solution)/shard_map/ppermute | solution.py:403
  21.6 2.9 %collective-permute-start.17 = (bf16[400,128]{1,0:T(8,128)(2,1)S(1)}, bf16[400,128]{1,0:T(8,128)(2,1)S(1)}, u32[]{:S(2)}, u32[]{:S(2)}) collective-permute-start(bf16[400,128]{1,0:T(8,128)(2,1)S(1)} %get-tuple-element.40), channel_id=1, source_target_pairs={{0,3},{1,6},{2,9},{3,12},{16,19},{17,22},{18,25},{19,28}} | collective-permute-start | bytes 307208 | tf_op jit(solution)/shard_map/ppermute | solution.py:403
  24.7 0.4 invert.1.index_ref
  25.1 3.5 %one_columns.1 = (bf16[37,16,128]{2,1,0:T(8,128)(2,1)S(1)}, bf16[37,16,128]{2,1,0:T(8,128)(2,1)S(1)}, bf16[37,16,128]{2,1,0:T(8,128)(2,1)S(1)}, bf16[37,16,128]{2,1,0:T(8,128)(2,1)S(1)}) custom-call(s32[8,128]{1,0:T(8,128)S(1)} %invert.1.index_ref, bf16[400,128]{1,0:T(8,128)(2,1)S(1)} %get-tuple-element.31.refs_0_, ...), custom_call_target="tpu_custom_call" | custom-call | flops 12000000 | bytes 4000000 | tf_op jit(solution)/shard_map/one_columns/pallas_call | solution.py:227
  28.6 3.7 %one_rows.1 = (bf16[37,16,128]{2,1,0:T(8,128)(2,1)S(1)}, bf16[37,16,128]{2,1,0:T(8,128)(2,1)S(1)}, bf16[37,16,128]{2,1,0:T(8,128)(2,1)S(1)}, bf16[37,16,128]{2,1,0:T(8,128)(2,1)S(1)}) custom-call(s32[64,6]{1,0:T(8,128)S(1)} %copy.6.cols_ref.index_ref, bf16[400,128]{1,0:T(8,128)(2,1)S(1)} %collective-permute-done.14.refs_0_, ...), custom_call_target="tpu_custom_call" | custom-call | flops 12000000 | bytes 4000000 | tf_op jit(solution)/shard_map/one_rows/pallas_call | solution.py:227
  32.4 2.9 %collective-permute-start.19 = (bf16[37,16,128]{2,1,0:T(8,128)(2,1)S(1)}, bf16[37,16,128]{2,1,0:T(8,128)(2,1)S(1)}, u32[]{:S(2)}, u32[]{:S(2)}) collective-permute-start(bf16[37,16,128]{2,1,0:T(8,128)(2,1)S(1)} %get-tuple-element.47), channel_id=1, source_target_pairs={{0,8},{4,12},{8,0},{12,4},{1,9},{5,13},{9,1},{13,5},{2,10},{6,14},... | collective-permute-start | bytes 454664 | tf_op jit(solution)/shard_map/ppermute | solution.py:414
  35.3 1.1 collective-permute-start.20
  36.4 2.8 %collective-permute-done.18.refs_1_ = bf16[37,16,128]{2,1,0:T(8,128)(2,1)S(1)} collective-permute-done((bf16[37,16,128]{2,1,0:T(8,128)(2,1)S(1)}, bf16[37,16,128]{2,1,0:T(8,128)(2,1)S(1)}, u32[]{:S(2)}, u32[]{:S(2)}) %collective-permute-start.18) | collective-permute-done | bytes 151584 | tf_op jit(solution)/shard_map/ppermute | solution.py:414
  39.2 1.7 %collective-permute-done.19.refs_2_ = bf16[37,16,128]{2,1,0:T(8,128)(2,1)S(1)} collective-permute-done((bf16[37,16,128]{2,1,0:T(8,128)(2,1)S(1)}, bf16[37,16,128]{2,1,0:T(8,128)(2,1)S(1)}, u32[]{:S(2)}, u32[]{:S(2)}) %collective-permute-start.19) | collective-permute-done | bytes 151584 | tf_op jit(solution)/shard_map/ppermute | solution.py:414
  40.9 1.5 %collective-permute-done.20.refs_3_ = bf16[37,16,128]{2,1,0:T(8,128)(2,1)S(1)} collective-permute-done((bf16[37,16,128]{2,1,0:T(8,128)(2,1)S(1)}, bf16[37,16,128]{2,1,0:T(8,128)(2,1)S(1)}, u32[]{:S(2)}, u32[]{:S(2)}) %collective-permute-start.20) | collective-permute-done | bytes 151584 | tf_op jit(solution)/shard_map/ppermute | solution.py:414
  42.3 1.1 merge.3.refs_0_
  43.5 0.9 collective-permute-start.21
  44.4 2.1 %collective-permute-start.5 = (bf16[37,16,128]{2,1,0:T(8,128)(2,1)S(1)}, bf16[37,16,128]{2,1,0:T(8,128)(2,1)S(1)}, u32[]{:S(2)}, u32[]{:S(2)}) collective-permute-start(bf16[37,16,128]{2,1,0:T(8,128)(2,1)S(1)} %get-tuple-element.33), channel_id=1, source_target_pairs={{0,1},{1,0},{2,3},{3,2},{4,5},{5,4},{6,7},{7,6},{8,9},{9,8},{10,11... | collective-permute-start | bytes 454664 | tf_op jit(solution)/shard_map/ppermute | solution.py:414
  46.5 2.4 %collective-permute-start.7 = (bf16[37,16,128]{2,1,0:T(8,128)(2,1)S(1)}, bf16[37,16,128]{2,1,0:T(8,128)(2,1)S(1)}, u32[]{:S(2)}, u32[]{:S(2)}) collective-permute-start(bf16[37,16,128]{2,1,0:T(8,128)(2,1)S(1)} %get-tuple-element.35), channel_id=1, source_target_pairs={{0,3},{1,2},{2,1},{3,0},{4,7},{5,6},{6,5},{7,4},{8,11},{9,10},{10,... | collective-permute-start | bytes 454664 | tf_op jit(solution)/shard_map/ppermute | solution.py:414
  48.8 1.7 %collective-permute-start.22 = (bf16[64,16,128]{2,1,0:T(8,128)(2,1)S(1)}, bf16[64,16,128]{2,1,0:T(8,128)(2,1)S(1)}, u32[]{:S(2)}, u32[]{:S(2)}) collective-permute-start(bf16[64,16,128]{2,1,0:T(8,128)(2,1)S(1)} %merge.3.refs_0_), channel_id=1, source_target_pairs={{0,8},{4,12},{8,0},{12,4},{1,9},{5,13},{9,1},{13,5},{2,10},{6,14},... | collective-permute-start | bytes 786440 | tf_op jit(solution)/shard_map/ppermute | solution.py:414
  50.5 0.4 collective-permute-done.5.refs_1_
  51.0 1.3 %collective-permute-start.23 = (bf16[64,16,128]{2,1,0:T(8,128)(2,1)S(1)}, bf16[64,16,128]{2,1,0:T(8,128)(2,1)S(1)}, u32[]{:S(2)}, u32[]{:S(2)}) collective-permute-start(bf16[64,16,128]{2,1,0:T(8,128)(2,1)S(1)} %merge.3.refs_0_), channel_id=1, source_target_pairs={{0,12},{4,8},{8,4},{12,0},{1,13},{5,9},{9,5},{13,1},{2,14},{6,10},... | collective-permute-start | bytes 786440 | tf_op jit(solution)/shard_map/ppermute | solution.py:414
  52.3 6.8 %collective-permute-done.6.refs_2_ = bf16[37,16,128]{2,1,0:T(8,128)(2,1)S(1)} collective-permute-done((bf16[37,16,128]{2,1,0:T(8,128)(2,1)S(1)}, bf16[37,16,128]{2,1,0:T(8,128)(2,1)S(1)}, u32[]{:S(2)}, u32[]{:S(2)}) %collective-permute-start.6) | collective-permute-done | bytes 151584 | tf_op jit(solution)/shard_map/ppermute | solution.py:414
  59.1 1.1 merge.2.refs_0_
  60.2 1.4 %collective-permute-start.10 = (bf16[64,16,128]{2,1,0:T(8,128)(2,1)S(1)}, bf16[64,16,128]{2,1,0:T(8,128)(2,1)S(1)}, u32[]{:S(2)}, u32[]{:S(2)}) collective-permute-start(bf16[64,16,128]{2,1,0:T(8,128)(2,1)S(1)} %merge.2.refs_0_), channel_id=1, source_target_pairs={{0,3},{1,2},{2,1},{3,0},{4,7},{5,6},{6,5},{7,4},{8,11},{9,10},{10,... | collective-permute-start | bytes 786440 | tf_op jit(solution)/shard_map/ppermute | solution.py:414
  61.6 4.7 %collective-permute-start.8 = (bf16[64,16,128]{2,1,0:T(8,128)(2,1)S(1)}, bf16[64,16,128]{2,1,0:T(8,128)(2,1)S(1)}, u32[]{:S(2)}, u32[]{:S(2)}) collective-permute-start(bf16[64,16,128]{2,1,0:T(8,128)(2,1)S(1)} %merge.2.refs_0_), channel_id=1, source_target_pairs={{0,1},{1,0},{2,3},{3,2},{4,5},{5,4},{6,7},{7,6},{8,9},{9,8},{10,11... | collective-permute-start | bytes 786440 | tf_op jit(solution)/shard_map/ppermute | solution.py:414
  66.3 0.5 collective-permute-start.9
  66.8 4.6 %assemble.1.slab_ref = bf16[64,6,128,128]{3,2,1,0:T(8,128)(2,1)S(1)} custom-call(bf16[32,6,128,128]{3,2,1,0:T(8,128)(2,1)} %bitcast.14, bf16[32,6,128,128]{3,2,1,0:T(8,128)(2,1)} %collective-permute-done.1.refs_1_.refs_5_), custom_call_target="tpu_custom_call" | custom-call | flops 4000000 | bytes 25000000 | tf_op jit(solution)/shard_map/assemble/pallas_call | solution.py:37
  71.4 4.7 %two_rows.1 = (bf16[64,16,128]{2,1,0:T(8,128)(2,1)S(1)}, bf16[64,16,128]{2,1,0:T(8,128)(2,1)S(1)}, bf16[64,16,128]{2,1,0:T(8,128)(2,1)S(1)}, bf16[64,16,128]{2,1,0:T(8,128)(2,1)S(1)}) custom-call(s32[64,6]{1,0:T(8,128)S(1)} %copy.6.cols_ref.index_ref, bf16[64,6,128,128]{3,2,1,0:T(8,128)(2,1)S(1)} %assemble.1.slab_ref, ...), custom_call_target="tpu_custom_call" | custom-call | flops 30000000 | bytes 12000000 | tf_op jit(solution)/shard_map/two_rows/pallas_call | solution.py:337
  76.3 3.4 %collective-permute-start.26 = (bf16[64,16,128]{2,1,0:T(8,128)(2,1)S(1)}, bf16[64,16,128]{2,1,0:T(8,128)(2,1)S(1)}, u32[]{:S(2)}, u32[]{:S(2)}) collective-permute-start(bf16[64,16,128]{2,1,0:T(8,128)(2,1)S(1)} %get-tuple-element.52), channel_id=1, source_target_pairs={{0,12},{4,8},{8,4},{12,0},{1,13},{5,9},{9,5},{13,1},{2,14},{6,10},... | collective-permute-start | bytes 786440 | tf_op jit(solution)/shard_map/ppermute | solution.py:414
  79.7 5.7 %collective-permute-done.9.refs_2_ = bf16[64,16,128]{2,1,0:T(8,128)(2,1)S(1)} collective-permute-done((bf16[64,16,128]{2,1,0:T(8,128)(2,1)S(1)}, bf16[64,16,128]{2,1,0:T(8,128)(2,1)S(1)}, u32[]{:S(2)}, u32[]{:S(2)}) %collective-permute-start.9) | collective-permute-done | bytes 262176 | tf_op jit(solution)/shard_map/ppermute | solution.py:414
  85.3 3.3 %two_columns.1 = (bf16[64,16,128]{2,1,0:T(8,128)(2,1)S(1)}, bf16[64,16,128]{2,1,0:T(8,128)(2,1)S(1)}, bf16[64,16,128]{2,1,0:T(8,128)(2,1)S(1)}, bf16[64,16,128]{2,1,0:T(8,128)(2,1)S(1)}) custom-call(s32[8,128]{1,0:T(8,128)S(1)} %invert.1.index_ref, bf16[64,6,128,128]{3,2,1,0:T(8,128)(2,1)S(1)} %assemble.1.slab_ref, bf16[64,16,128]{2,1,0:T(8,128)(2,1)S(1)} %merge.2.refs_0_, ...), custom_call_target="tpu_custom_call" | custom-call | flops 30000000 | bytes 12000000 | tf_op jit(solution)/shard_map/two_columns/pallas_call | solution.py:337
  88.7 1.9 %collective-permute-start.12 = (bf16[64,16,128]{2,1,0:T(8,128)(2,1)S(1)}, bf16[64,16,128]{2,1,0:T(8,128)(2,1)S(1)}, u32[]{:S(2)}, u32[]{:S(2)}) collective-permute-start(bf16[64,16,128]{2,1,0:T(8,128)(2,1)S(1)} %get-tuple-element.38), channel_id=1, source_target_pairs={{0,8},{4,12},{8,0},{12,4},{1,9},{5,13},{9,1},{13,5},{2,10},{6,14},... | collective-permute-start | bytes 786440 | tf_op jit(solution)/shard_map/ppermute | solution.py:414
  90.6 1.5 %collective-permute-start.13 = (bf16[64,16,128]{2,1,0:T(8,128)(2,1)S(1)}, bf16[64,16,128]{2,1,0:T(8,128)(2,1)S(1)}, u32[]{:S(2)}, u32[]{:S(2)}) collective-permute-start(bf16[64,16,128]{2,1,0:T(8,128)(2,1)S(1)} %get-tuple-element.39), channel_id=1, source_target_pairs={{0,12},{4,8},{8,4},{12,0},{1,13},{5,9},{9,5},{13,1},{2,14},{6,10},... | collective-permute-start | bytes 786440 | tf_op jit(solution)/shard_map/ppermute | solution.py:414
  92.2 0.1 pick.1
  92.4 1.8 %collective-permute-start.28 = (bf16[64,16,128]{2,1,0:T(8,128)(2,1)S(1)}, bf16[64,16,128]{2,1,0:T(8,128)(2,1)S(1)}, u32[]{:S(2)}, u32[]{:S(2)}) collective-permute-start(bf16[64,16,128]{2,1,0:T(8,128)(2,1)S(1)} %get-tuple-element.55), channel_id=1, source_target_pairs={{0,2},{1,3},{2,0},{3,1},{4,6},{5,7},{6,4},{7,5},{8,10},{9,11},{10,... | collective-permute-start | bytes 786440 | tf_op jit(solution)/shard_map/ppermute | solution.py:414
  94.2 3.6 %collective-permute-done.11.refs_1_ = bf16[64,16,128]{2,1,0:T(8,128)(2,1)S(1)} collective-permute-done((bf16[64,16,128]{2,1,0:T(8,128)(2,1)S(1)}, bf16[64,16,128]{2,1,0:T(8,128)(2,1)S(1)}, u32[]{:S(2)}, u32[]{:S(2)}) %collective-permute-start.11) | collective-permute-done | bytes 262176 | tf_op jit(solution)/shard_map/ppermute | solution.py:414
  97.9 1.3 %collective-permute-start.29 = (bf16[64,16,128]{2,1,0:T(8,128)(2,1)S(1)}, bf16[64,16,128]{2,1,0:T(8,128)(2,1)S(1)}, u32[]{:S(2)}, u32[]{:S(2)}) collective-permute-start(bf16[64,16,128]{2,1,0:T(8,128)(2,1)S(1)} %get-tuple-element.56), channel_id=1, source_target_pairs={{0,3},{1,2},{2,1},{3,0},{4,7},{5,6},{6,5},{7,4},{8,11},{9,10},{10,... | collective-permute-start | bytes 786440 | tf_op jit(solution)/shard_map/ppermute | solution.py:414
  99.1 2.5 %collective-permute-done.12.refs_2_ = bf16[64,16,128]{2,1,0:T(8,128)(2,1)S(1)} collective-permute-done((bf16[64,16,128]{2,1,0:T(8,128)(2,1)S(1)}, bf16[64,16,128]{2,1,0:T(8,128)(2,1)S(1)}, u32[]{:S(2)}, u32[]{:S(2)}) %collective-permute-start.12) | collective-permute-done | bytes 262176 | tf_op jit(solution)/shard_map/ppermute | solution.py:414
  101.7 1.4 %collective-permute-done.13.refs_3_ = bf16[64,16,128]{2,1,0:T(8,128)(2,1)S(1)} collective-permute-done((bf16[64,16,128]{2,1,0:T(8,128)(2,1)S(1)}, bf16[64,16,128]{2,1,0:T(8,128)(2,1)S(1)}, u32[]{:S(2)}, u32[]{:S(2)}) %collective-permute-start.13) | collective-permute-done | bytes 262176 | tf_op jit(solution)/shard_map/ppermute | solution.py:414
  103.1 1.0 finish.2.refs_0_
  104.1 9.7 %collective-permute-done.28.refs_3_ = bf16[64,16,128]{2,1,0:T(8,128)(2,1)S(1)} collective-permute-done((bf16[64,16,128]{2,1,0:T(8,128)(2,1)S(1)}, bf16[64,16,128]{2,1,0:T(8,128)(2,1)S(1)}, u32[]{:S(2)}, u32[]{:S(2)}) %collective-permute-start.28) | collective-permute-done | bytes 262176 | tf_op jit(solution)/shard_map/ppermute | solution.py:414
  113.8 1.1 finish.3
  (27 shorter events, 0.6 us)
Async XLA Ops:
  0.0 25.1 %collective-permute-start.1 = (bf16[32,6,128,128]{3,2,1,0:T(8,128)(2,1)}, bf16[32,6,128,128]{3,2,1,0:T(8,128)(2,1)}, u32[]{:S(2)}, u32[]{:S(2)}) collective-permute-start(bf16[32,6,128,128]{3,2,1,0:T(8,128)(2,1)} %bitcast.10), channel_id=1, source_target_pairs={{16,0},{0,16},{17,1},{1,17},{18,2},{2,18},{19,3},{3,19},{20,4},{4,... | collective-permute-start | bytes 18874376 | tf_op jit(solution)/shard_map/ppermute | solution.py:400
  2.1 9.1 %collective-permute-start.2 = (bf16[400,128]{1,0:T(8,128)(2,1)S(1)}, bf16[400,128]{1,0:T(8,128)(2,1)S(1)}, u32[]{:S(2)}, u32[]{:S(2)}) collective-permute-start(bf16[400,128]{1,0:T(8,128)(2,1)S(1)} %get-tuple-element.31.refs_0_), channel_id=1, source_target_pairs={{0,4},{1,5},{2,6},{3,7},{16,20},{17,21},{18,22},{19,23}} | collective-permute-start | bytes 307208 | tf_op jit(solution)/shard_map/ppermute | solution.py:406
  6.5 12.3 %collective-permute-start.3 = (bf16[400,128]{1,0:T(8,128)(2,1)S(1)}, bf16[400,128]{1,0:T(8,128)(2,1)S(1)}, u32[]{:S(2)}, u32[]{:S(2)}) collective-permute-start(bf16[400,128]{1,0:T(8,128)(2,1)S(1)} %get-tuple-element.31.refs_0_), channel_id=1, source_target_pairs={{0,8},{1,9},{2,10},{3,11},{16,24},{17,25},{18,26},{19,27}} | collective-permute-start | bytes 307208 | tf_op jit(solution)/shard_map/ppermute | solution.py:406
  7.8 13.8 %collective-permute-start.4 = (bf16[400,128]{1,0:T(8,128)(2,1)S(1)}, bf16[400,128]{1,0:T(8,128)(2,1)S(1)}, u32[]{:S(2)}, u32[]{:S(2)}) collective-permute-start(bf16[400,128]{1,0:T(8,128)(2,1)S(1)} %get-tuple-element.31.refs_0_), channel_id=1, source_target_pairs={{0,12},{1,13},{2,14},{3,15},{16,28},{17,29},{18,30},{19,31}} | collective-permute-start | bytes 307208 | tf_op jit(solution)/shard_map/ppermute | solution.py:406
  9.1 1.5 %collective-permute-start = (s32[32,6]{0,1:T(8,128)S(1)}, s32[32,6]{0,1:T(8,128)S(1)}, u32[]{:S(2)}, u32[]{:S(2)}) collective-permute-start(s32[32,6]{0,1:T(8,128)S(1)} %bitcast.8), channel_id=1, source_target_pairs={{16,0},{0,16},{17,1},{1,17},{18,2},{2,18},{19,3},{3,19},{20,4},{4,... | collective-permute-start | bytes 2312 | tf_op jit(solution)/shard_map/ppermute | solution.py:399
  10.6 17.9 %collective-permute-start.14 = (bf16[400,128]{1,0:T(8,128)(2,1)S(1)}, bf16[400,128]{1,0:T(8,128)(2,1)S(1)}, u32[]{:S(2)}, u32[]{:S(2)}) collective-permute-start(bf16[400,128]{1,0:T(8,128)(2,1)S(1)} %get-tuple-element.40), channel_id=1, source_target_pairs={{0,0},{1,5},{2,10},{3,15},{16,16},{17,21},{18,26},{19,31}} | collective-permute-start | bytes 307208 | tf_op jit(solution)/shard_map/ppermute | solution.py:403
  11.3 17.3 %collective-permute-start.15 = (bf16[400,128]{1,0:T(8,128)(2,1)S(1)}, bf16[400,128]{1,0:T(8,128)(2,1)S(1)}, u32[]{:S(2)}, u32[]{:S(2)}) collective-permute-start(bf16[400,128]{1,0:T(8,128)(2,1)S(1)} %get-tuple-element.40), channel_id=1, source_target_pairs={{0,1},{1,4},{2,11},{3,14},{16,17},{17,20},{18,27},{19,30}} | collective-permute-start | bytes 307208 | tf_op jit(solution)/shard_map/ppermute | solution.py:403
  18.9 9.7 %collective-permute-start.16 = (bf16[400,128]{1,0:T(8,128)(2,1)S(1)}, bf16[400,128]{1,0:T(8,128)(2,1)S(1)}, u32[]{:S(2)}, u32[]{:S(2)}) collective-permute-start(bf16[400,128]{1,0:T(8,128)(2,1)S(1)} %get-tuple-element.40), channel_id=1, source_target_pairs={{0,2},{1,7},{2,8},{3,13},{16,18},{17,23},{18,24},{19,29}} | collective-permute-start | bytes 307208 | tf_op jit(solution)/shard_map/ppermute | solution.py:403
  21.6 7.0 %collective-permute-start.17 = (bf16[400,128]{1,0:T(8,128)(2,1)S(1)}, bf16[400,128]{1,0:T(8,128)(2,1)S(1)}, u32[]{:S(2)}, u32[]{:S(2)}) collective-permute-start(bf16[400,128]{1,0:T(8,128)(2,1)S(1)} %get-tuple-element.40), channel_id=1, source_target_pairs={{0,3},{1,6},{2,9},{3,12},{16,19},{17,22},{18,25},{19,28}} | collective-permute-start | bytes 307208 | tf_op jit(solution)/shard_map/ppermute | solution.py:403
  32.3 6.9 %collective-permute-start.18 = (bf16[37,16,128]{2,1,0:T(8,128)(2,1)S(1)}, bf16[37,16,128]{2,1,0:T(8,128)(2,1)S(1)}, u32[]{:S(2)}, u32[]{:S(2)}) collective-permute-start(bf16[37,16,128]{2,1,0:T(8,128)(2,1)S(1)} %get-tuple-element.46), channel_id=1, source_target_pairs={{0,4},{4,0},{8,12},{12,8},{1,5},{5,1},{9,13},{13,9},{2,6},{6,2},{1... | collective-permute-start | bytes 454664 | tf_op jit(solution)/shard_map/ppermute | solution.py:414
  32.4 8.5 %collective-permute-start.19 = (bf16[37,16,128]{2,1,0:T(8,128)(2,1)S(1)}, bf16[37,16,128]{2,1,0:T(8,128)(2,1)S(1)}, u32[]{:S(2)}, u32[]{:S(2)}) collective-permute-start(bf16[37,16,128]{2,1,0:T(8,128)(2,1)S(1)} %get-tuple-element.47), channel_id=1, source_target_pairs={{0,8},{4,12},{8,0},{12,4},{1,9},{5,13},{9,1},{13,5},{2,10},{6,14},... | collective-permute-start | bytes 454664 | tf_op jit(solution)/shard_map/ppermute | solution.py:414
  35.3 7.0 %collective-permute-start.20 = (bf16[37,16,128]{2,1,0:T(8,128)(2,1)S(1)}, bf16[37,16,128]{2,1,0:T(8,128)(2,1)S(1)}, u32[]{:S(2)}, u32[]{:S(2)}) collective-permute-start(bf16[37,16,128]{2,1,0:T(8,128)(2,1)S(1)} %get-tuple-element.48), channel_id=1, source_target_pairs={{0,12},{4,8},{8,4},{12,0},{1,13},{5,9},{9,5},{13,1},{2,14},{6,10},... | collective-permute-start | bytes 454664 | tf_op jit(solution)/shard_map/ppermute | solution.py:414
  43.5 22.8 %collective-permute-start.21 = (bf16[64,16,128]{2,1,0:T(8,128)(2,1)S(1)}, bf16[64,16,128]{2,1,0:T(8,128)(2,1)S(1)}, u32[]{:S(2)}, u32[]{:S(2)}) collective-permute-start(bf16[64,16,128]{2,1,0:T(8,128)(2,1)S(1)} %merge.3.refs_0_), channel_id=1, source_target_pairs={{0,4},{4,0},{8,12},{12,8},{1,5},{5,1},{9,13},{13,9},{2,6},{6,2},{1... | collective-permute-start | bytes 786440 | tf_op jit(solution)/shard_map/ppermute | solution.py:414
  44.4 6.6 %collective-permute-start.5 = (bf16[37,16,128]{2,1,0:T(8,128)(2,1)S(1)}, bf16[37,16,128]{2,1,0:T(8,128)(2,1)S(1)}, u32[]{:S(2)}, u32[]{:S(2)}) collective-permute-start(bf16[37,16,128]{2,1,0:T(8,128)(2,1)S(1)} %get-tuple-element.33), channel_id=1, source_target_pairs={{0,1},{1,0},{2,3},{3,2},{4,5},{5,4},{6,7},{7,6},{8,9},{9,8},{10,11... | collective-permute-start | bytes 454664 | tf_op jit(solution)/shard_map/ppermute | solution.py:414
  46.5 12.6 %collective-permute-start.6 = (bf16[37,16,128]{2,1,0:T(8,128)(2,1)S(1)}, bf16[37,16,128]{2,1,0:T(8,128)(2,1)S(1)}, u32[]{:S(2)}, u32[]{:S(2)}) collective-permute-start(bf16[37,16,128]{2,1,0:T(8,128)(2,1)S(1)} %get-tuple-element.34), channel_id=1, source_target_pairs={{0,2},{1,3},{2,0},{3,1},{4,6},{5,7},{6,4},{7,5},{8,10},{9,11},{10,... | collective-permute-start | bytes 454664 | tf_op jit(solution)/shard_map/ppermute | solution.py:414
  46.5 12.6 %collective-permute-start.7 = (bf16[37,16,128]{2,1,0:T(8,128)(2,1)S(1)}, bf16[37,16,128]{2,1,0:T(8,128)(2,1)S(1)}, u32[]{:S(2)}, u32[]{:S(2)}) collective-permute-start(bf16[37,16,128]{2,1,0:T(8,128)(2,1)S(1)} %get-tuple-element.35), channel_id=1, source_target_pairs={{0,3},{1,2},{2,1},{3,0},{4,7},{5,6},{6,5},{7,4},{8,11},{9,10},{10,... | collective-permute-start | bytes 454664 | tf_op jit(solution)/shard_map/ppermute | solution.py:414
  48.8 22.6 %collective-permute-start.22 = (bf16[64,16,128]{2,1,0:T(8,128)(2,1)S(1)}, bf16[64,16,128]{2,1,0:T(8,128)(2,1)S(1)}, u32[]{:S(2)}, u32[]{:S(2)}) collective-permute-start(bf16[64,16,128]{2,1,0:T(8,128)(2,1)S(1)} %merge.3.refs_0_), channel_id=1, source_target_pairs={{0,8},{4,12},{8,0},{12,4},{1,9},{5,13},{9,1},{13,5},{2,10},{6,14},... | collective-permute-start | bytes 786440 | tf_op jit(solution)/shard_map/ppermute | solution.py:414
  51.0 20.4 %collective-permute-start.23 = (bf16[64,16,128]{2,1,0:T(8,128)(2,1)S(1)}, bf16[64,16,128]{2,1,0:T(8,128)(2,1)S(1)}, u32[]{:S(2)}, u32[]{:S(2)}) collective-permute-start(bf16[64,16,128]{2,1,0:T(8,128)(2,1)S(1)} %merge.3.refs_0_), channel_id=1, source_target_pairs={{0,12},{4,8},{8,4},{12,0},{1,13},{5,9},{9,5},{13,1},{2,14},{6,10},... | collective-permute-start | bytes 786440 | tf_op jit(solution)/shard_map/ppermute | solution.py:414
  60.2 16.0 %collective-permute-start.10 = (bf16[64,16,128]{2,1,0:T(8,128)(2,1)S(1)}, bf16[64,16,128]{2,1,0:T(8,128)(2,1)S(1)}, u32[]{:S(2)}, u32[]{:S(2)}) collective-permute-start(bf16[64,16,128]{2,1,0:T(8,128)(2,1)S(1)} %merge.2.refs_0_), channel_id=1, source_target_pairs={{0,3},{1,2},{2,1},{3,0},{4,7},{5,6},{6,5},{7,4},{8,11},{9,10},{10,... | collective-permute-start | bytes 786440 | tf_op jit(solution)/shard_map/ppermute | solution.py:414
  61.6 18.0 %collective-permute-start.8 = (bf16[64,16,128]{2,1,0:T(8,128)(2,1)S(1)}, bf16[64,16,128]{2,1,0:T(8,128)(2,1)S(1)}, u32[]{:S(2)}, u32[]{:S(2)}) collective-permute-start(bf16[64,16,128]{2,1,0:T(8,128)(2,1)S(1)} %merge.2.refs_0_), channel_id=1, source_target_pairs={{0,1},{1,0},{2,3},{3,2},{4,5},{5,4},{6,7},{7,6},{8,9},{9,8},{10,11... | collective-permute-start | bytes 786440 | tf_op jit(solution)/shard_map/ppermute | solution.py:414
  66.3 19.0 %collective-permute-start.9 = (bf16[64,16,128]{2,1,0:T(8,128)(2,1)S(1)}, bf16[64,16,128]{2,1,0:T(8,128)(2,1)S(1)}, u32[]{:S(2)}, u32[]{:S(2)}) collective-permute-start(bf16[64,16,128]{2,1,0:T(8,128)(2,1)S(1)} %merge.2.refs_0_), channel_id=1, source_target_pairs={{0,2},{1,3},{2,0},{3,1},{4,6},{5,7},{6,4},{7,5},{8,10},{9,11},{10,... | collective-permute-start | bytes 786440 | tf_op jit(solution)/shard_map/ppermute | solution.py:414
  76.1 14.5 %collective-permute-start.24 = (bf16[64,16,128]{2,1,0:T(8,128)(2,1)S(1)}, bf16[64,16,128]{2,1,0:T(8,128)(2,1)S(1)}, u32[]{:S(2)}, u32[]{:S(2)}) collective-permute-start(bf16[64,16,128]{2,1,0:T(8,128)(2,1)S(1)} %get-tuple-element.50), channel_id=1, source_target_pairs={{0,4},{4,0},{8,12},{12,8},{1,5},{5,1},{9,13},{13,9},{2,6},{6,2},{1... | collective-permute-start | bytes 786440 | tf_op jit(solution)/shard_map/ppermute | solution.py:414
  76.2 16.0 %collective-permute-start.25 = (bf16[64,16,128]{2,1,0:T(8,128)(2,1)S(1)}, bf16[64,16,128]{2,1,0:T(8,128)(2,1)S(1)}, u32[]{:S(2)}, u32[]{:S(2)}) collective-permute-start(bf16[64,16,128]{2,1,0:T(8,128)(2,1)S(1)} %get-tuple-element.51), channel_id=1, source_target_pairs={{0,8},{4,12},{8,0},{12,4},{1,9},{5,13},{9,1},{13,5},{2,10},{6,14},... | collective-permute-start | bytes 786440 | tf_op jit(solution)/shard_map/ppermute | solution.py:414
  76.3 15.9 %collective-permute-start.26 = (bf16[64,16,128]{2,1,0:T(8,128)(2,1)S(1)}, bf16[64,16,128]{2,1,0:T(8,128)(2,1)S(1)}, u32[]{:S(2)}, u32[]{:S(2)}) collective-permute-start(bf16[64,16,128]{2,1,0:T(8,128)(2,1)S(1)} %get-tuple-element.52), channel_id=1, source_target_pairs={{0,12},{4,8},{8,4},{12,0},{1,13},{5,9},{9,5},{13,1},{2,14},{6,10},... | collective-permute-start | bytes 786440 | tf_op jit(solution)/shard_map/ppermute | solution.py:414
  88.6 9.2 %collective-permute-start.11 = (bf16[64,16,128]{2,1,0:T(8,128)(2,1)S(1)}, bf16[64,16,128]{2,1,0:T(8,128)(2,1)S(1)}, u32[]{:S(2)}, u32[]{:S(2)}) collective-permute-start(bf16[64,16,128]{2,1,0:T(8,128)(2,1)S(1)} %get-tuple-element.37), channel_id=1, source_target_pairs={{0,4},{4,0},{8,12},{12,8},{1,5},{5,1},{9,13},{13,9},{2,6},{6,2},{1... | collective-permute-start | bytes 786440 | tf_op jit(solution)/shard_map/ppermute | solution.py:414
  88.7 13.0 %collective-permute-start.12 = (bf16[64,16,128]{2,1,0:T(8,128)(2,1)S(1)}, bf16[64,16,128]{2,1,0:T(8,128)(2,1)S(1)}, u32[]{:S(2)}, u32[]{:S(2)}) collective-permute-start(bf16[64,16,128]{2,1,0:T(8,128)(2,1)S(1)} %get-tuple-element.38), channel_id=1, source_target_pairs={{0,8},{4,12},{8,0},{12,4},{1,9},{5,13},{9,1},{13,5},{2,10},{6,14},... | collective-permute-start | bytes 786440 | tf_op jit(solution)/shard_map/ppermute | solution.py:414
  90.6 12.5 %collective-permute-start.13 = (bf16[64,16,128]{2,1,0:T(8,128)(2,1)S(1)}, bf16[64,16,128]{2,1,0:T(8,128)(2,1)S(1)}, u32[]{:S(2)}, u32[]{:S(2)}) collective-permute-start(bf16[64,16,128]{2,1,0:T(8,128)(2,1)S(1)} %get-tuple-element.39), channel_id=1, source_target_pairs={{0,12},{4,8},{8,4},{12,0},{1,13},{5,9},{9,5},{13,1},{2,14},{6,10},... | collective-permute-start | bytes 786440 | tf_op jit(solution)/shard_map/ppermute | solution.py:414
  92.3 11.8 %collective-permute-start.27 = (bf16[64,16,128]{2,1,0:T(8,128)(2,1)S(1)}, bf16[64,16,128]{2,1,0:T(8,128)(2,1)S(1)}, u32[]{:S(2)}, u32[]{:S(2)}) collective-permute-start(bf16[64,16,128]{2,1,0:T(8,128)(2,1)S(1)} %get-tuple-element.54), channel_id=1, source_target_pairs={{0,1},{1,0},{2,3},{3,2},{4,5},{5,4},{6,7},{7,6},{8,9},{9,8},{10,11... | collective-permute-start | bytes 786440 | tf_op jit(solution)/shard_map/ppermute | solution.py:414
  92.4 21.4 %collective-permute-start.28 = (bf16[64,16,128]{2,1,0:T(8,128)(2,1)S(1)}, bf16[64,16,128]{2,1,0:T(8,128)(2,1)S(1)}, u32[]{:S(2)}, u32[]{:S(2)}) collective-permute-start(bf16[64,16,128]{2,1,0:T(8,128)(2,1)S(1)} %get-tuple-element.55), channel_id=1, source_target_pairs={{0,2},{1,3},{2,0},{3,1},{4,6},{5,7},{6,4},{7,5},{8,10},{9,11},{10,... | collective-permute-start | bytes 786440 | tf_op jit(solution)/shard_map/ppermute | solution.py:414
  97.9 15.9 %collective-permute-start.29 = (bf16[64,16,128]{2,1,0:T(8,128)(2,1)S(1)}, bf16[64,16,128]{2,1,0:T(8,128)(2,1)S(1)}, u32[]{:S(2)}, u32[]{:S(2)}) collective-permute-start(bf16[64,16,128]{2,1,0:T(8,128)(2,1)S(1)} %get-tuple-element.56), channel_id=1, source_target_pairs={{0,3},{1,2},{2,1},{3,0},{4,7},{5,6},{6,5},{7,4},{8,11},{9,10},{10,... | collective-permute-start | bytes 786440 | tf_op jit(solution)/shard_map/ppermute | solution.py:414
